TPU v7x, 8 devices: a whole 2x2x1 slice. The times are simulated.
8 devices in a mesh: tp: 8 (over z, y, x, core).
Axes of the slice: x: 2, y: 2, z: 1, core: 2. Of those that a mesh axis runs over, the one named last changes fastest.
Arguments:
- tok_ids: int32 [2, 512], replicated
- next_ids: int32 [2, 512], replicated
- seq_lens: int32 [512], replicated
- embed: bfloat16 [256000, 2048], P('tp')
- ln_gain: bfloat16 [2048], replicated
- w_in: bfloat16 [2048, 35328], P(None, 'tp')
- w_out: bfloat16 [18432, 2048], P('tp')
- final_gain: bfloat16 [2048], replicated
- k_cache: bfloat16 [512, 128, 256], P('tp')
- v_cache: bfloat16 [512, 128, 256], P('tp')
Outputs:
- output 1: float32 [2, 512], replicated
- output 2: bfloat16 [512, 128, 256], P('tp')
- output 3: bfloat16 [512, 128, 256], P('tp')
All inputs are finite; a program needn't handle non-finite values.
Results may differ from a plain program's by a relative error of at most 0.001.
Values are sent between devices in bfloat16 or wider.
A program may use at most 1 GiB of HBM per device.

v0:
```python
import functools
import math

import jax
import jax.numpy as jnp
from jax import lax
from jax.experimental import pallas as pl
from jax.experimental.pallas import tpu as pltpu
from jax.sharding import PartitionSpec as P

ROPE_BASE = 10000.0
NORM_EPS = 1e-6
LOG2E = 1.4426950408889634
MESH_ID = pl.DeviceIdType.MESH
F32 = jnp.float32
BF16 = jnp.bfloat16
MIB = 2 ** 20


def norm_rows(values, gain_row):
    centered = values - jnp.mean(values, axis=-1, keepdims=True)
    variance = jnp.mean(jnp.square(centered), axis=-1, keepdims=True)
    return (centered * lax.rsqrt(variance + NORM_EPS) * gain_row.astype(F32)).astype(BF16)


def gather_kernel(count, vocab_dev, ids_ref, embed_ref, out_ref, blocks, rows, wide, slots, sem):
    width = out_ref.shape[1]
    per_loop = 8

    def compact(idx, total):
        for sub in range(per_loop):
            pos = idx * per_loop + sub
            local_id = ids_ref[pos]
            slots[total] = pos
            total = total + jnp.where((local_id >= 0) & (local_id < vocab_dev), 1, 0)
        return total

    total = lax.fori_loop(0, count // per_loop, compact, jnp.int32(0))

    def block_copy(slot):
        local_id = ids_ref[slots[slot]]
        start = pl.multiple_of((local_id // 8) * 8, 8)
        return pltpu.make_async_copy(embed_ref.at[pl.ds(start, 8), :], blocks.at[slot], sem)

    def issue(slot, carry):
        block_copy(slot).start()
        return carry

    lax.fori_loop(0, total, issue, 0)
    rows[...] = jnp.zeros_like(rows)

    def drain(slot, carry):
        pltpu.make_async_copy(embed_ref.at[pl.ds(0, 8), :], blocks.at[slot], sem).wait()
        return carry

    lax.fori_loop(0, total, drain, 0)

    def pick(idx, carry):
        for sub in range(4):
            slot = idx * 4 + sub

            @pl.when(slot < total)
            def _():
                wide[sub] = blocks[slot].astype(F32)

        for sub in range(4):
            slot = idx * 4 + sub

            @pl.when(slot < total)
            def _():
                pos = slots[slot]
                rows[pl.ds(pos, 1), :] = wide[sub, pl.ds(lax.rem(ids_ref[pos], 8), 1), :]

        return carry

    lax.fori_loop(0, (total + 3) // 4, pick, 0)
    out_ref[...] = rows[...].astype(BF16)


def gather_rows(local_ids, embed_loc):
    count = local_ids.shape[0]
    vocab_dev, width = embed_loc.shape
    return pl.pallas_call(
        functools.partial(gather_kernel, count, vocab_dev),
        grid_spec=pltpu.PrefetchScalarGridSpec(
            num_scalar_prefetch=1,
            grid=(1,),
            in_specs=[pl.BlockSpec(memory_space=pl.ANY)],
            out_specs=pl.BlockSpec((count, width), lambda i, ids: (0, 0)),
            scratch_shapes=[
                pltpu.VMEM((count, 8, width), BF16),
                pltpu.VMEM((count, width), F32),
                pltpu.VMEM((4, 8, width), F32),
                pltpu.SMEM((count + 1,), jnp.int32),
                pltpu.SemaphoreType.DMA,
            ],
        ),
        out_shape=jax.ShapeDtypeStruct((count, width), BF16),
        compiler_params=pltpu.CompilerParams(vmem_limit_bytes=60 * MIB),
        name="gather_rows",
    )(local_ids, embed_loc)


def exchange_kernel(chunks, with_base, *refs):
    if with_base:
        part, base, gain, full, pair_buf, send_buf, recv_buf, pair_sems, sum_sems, own_sems, all_sems, fwd_sems = refs
        own = None
    else:
        part, gain, full, own, pair_buf, send_buf, recv_buf, pair_sems, sum_sems, own_sems, all_sems, fwd_sems = refs
    me = lax.axis_index("tp")
    chip, core = me // 2, lax.rem(me, 2)
    other = 1 - core
    mate = chip * 2 + other
    chips = [chip, lax.rem(chip, 2) * (-2) + chip + 1, lax.rem(chip + 2, 4), 3 - chip]
    peers = [chips[k] * 2 + core for k in range(4)]
    size = part.shape[2] // chunks

    barrier = pltpu.get_barrier_semaphore()
    for target in [mate] + peers[1:]:
        pl.semaphore_signal(barrier, inc=1, device_id=(target,), device_id_type=MESH_ID)
    pl.semaphore_wait(barrier, 4)

    def span(c):
        return pl.ds(c * size, size)

    def remote(src, dst, sems, idx, target):
        return pltpu.make_async_remote_copy(
            src_ref=src, dst_ref=dst, send_sem=sems.at[(0,) + idx], recv_sem=sems.at[(1,) + idx],
            device_id=(target,), device_id_type=MESH_ID)

    pair = [remote(part.at[:, other, span(c), :], pair_buf.at[:, span(c), :], pair_sems, (c,), mate) for c in range(chunks)]
    sums = [[remote(send_buf.at[k - 1, span(c), :], recv_buf.at[k - 1, span(c), :], sum_sems, (k - 1, c), peers[k])
             for c in range(chunks)] for k in (1, 2, 3)]
    mine = [full.at[chip, core, span(c), :] for c in range(chunks)]
    give = [remote(mine[c], mine[c], own_sems, (c,), mate) for c in range(chunks)]
    alls = [[remote(mine[c], mine[c], all_sems, (k - 1, c), peers[k]) for c in range(chunks)] for k in (1, 2, 3)]

    def landed(k, c):
        return full.at[chips[k], core, span(c), :]

    fwds = [[remote(landed(k, c), landed(k, c), fwd_sems, (k - 1, c), mate) for c in range(chunks)] for k in (1, 2, 3)]

    for c in range(chunks):
        pair[c].start()
    for c in range(chunks):
        pair[c].wait_recv()
        for k in (3, 1, 2):
            both = part[chips[k], core, span(c), :].astype(F32) + pair_buf[chips[k], span(c), :].astype(F32)
            send_buf[k - 1, span(c), :] = both.astype(BF16)
            sums[k - 1][c].start()
    for c in range(chunks):
        total = part[chip, core, span(c), :].astype(F32) + pair_buf[chip, span(c), :].astype(F32)
        for k in (1, 2, 3):
            sums[k - 1][c].wait_recv()
            total = total + recv_buf[k - 1, span(c), :].astype(F32)
        summed = total.astype(BF16)
        if with_base:
            rows = base[span(c), :].astype(F32) + summed.astype(F32)
        else:
            own[span(c), :] = summed
            rows = summed.astype(F32)
        full[chip, core, span(c), :] = norm_rows(rows, gain[...])
        for k in (3, 1, 2):
            alls[k - 1][c].start()
        give[c].start()
    for c in range(chunks):
        for k in (1, 2, 3):
            alls[k - 1][c].wait_recv()
            fwds[k - 1][c].start()
    for c in range(chunks):
        give[c].wait_recv()
        for k in (1, 2, 3):
            fwds[k - 1][c].wait_recv()
    for c in range(chunks):
        pair[c].wait_send()
        give[c].wait_send()
        for k in (0, 1, 2):
            sums[k][c].wait_send()
            alls[k][c].wait_send()
            fwds[k][c].wait_send()


def exchange(part, base, gain, cid, chunks=4):
    rows, width = part.shape
    own_rows = rows // 8
    vmem = pl.BlockSpec(memory_space=pltpu.VMEM)
    full_shape = jax.ShapeDtypeStruct((4, 2, own_rows, width), BF16)
    with_base = base is not None
    dma = pltpu.SemaphoreType.DMA
    args = [part.reshape(4, 2, own_rows, width)] + ([base] if with_base else []) + [gain.reshape(1, width)]
    out = pl.pallas_call(
        functools.partial(exchange_kernel, chunks, with_base),
        in_specs=[vmem] * len(args),
        out_specs=[vmem] if with_base else [vmem, vmem],
        out_shape=[full_shape] if with_base else [full_shape, jax.ShapeDtypeStruct((own_rows, width), BF16)],
        scratch_shapes=[
            pltpu.VMEM((4, own_rows, width), BF16),
            pltpu.VMEM((3, own_rows, width), BF16),
            pltpu.VMEM((3, own_rows, width), BF16),
            dma((2, chunks)), dma((2, 3, chunks)), dma((2, chunks)), dma((2, 3, chunks)), dma((2, 3, chunks)),
        ],
        compiler_params=pltpu.CompilerParams(collective_id=cid, has_side_effects=True, vmem_limit_bytes=40 * MIB),
        name="exchange_rows",
    )(*args)
    full = out[0].reshape(rows, width)
    return (full, None) if with_base else (full, out[1])


def attention_kernel(seqs, steps, heads, lens_ref, q_ref, kn_ref, vn_ref, k_ref, v_ref, o_ref, ko_ref, vo_ref):
    first = pl.program_id(0) * seqs
    cache_len = k_ref.shape[1]
    head_dim = k_ref.shape[2]
    times = lax.broadcasted_iota(jnp.int32, (cache_len, head_dim), 0)
    qtime = lax.broadcasted_iota(jnp.int32, (steps * heads, cache_len), 1)
    qstep = lax.broadcasted_iota(jnp.int32, (steps * heads, cache_len), 0) // heads
    for b in range(seqs):
        pos = lens_ref[first + b]
        kb = k_ref[b].astype(F32)
        vb = v_ref[b].astype(F32)
        for s in range(steps):
            hit = times == pos + s
            kb = jnp.where(hit, kn_ref[b, s:s + 1, :].astype(F32), kb)
            vb = jnp.where(hit, vn_ref[b, s:s + 1, :].astype(F32), vb)
        kb = kb.astype(BF16)
        vb = vb.astype(BF16)
        ko_ref[b] = kb
        vo_ref[b] = vb
        scores = lax.dot_general(q_ref[b], kb, (((1,), (1,)), ((), ())), preferred_element_type=F32)
        scores = jnp.where(qtime <= pos + qstep, scores, -jnp.inf)
        expd = jnp.exp(scores - jnp.max(scores, axis=-1, keepdims=True))
        probs = (expd / jnp.sum(expd, axis=-1, keepdims=True)).astype(BF16)
        o_ref[b] = jnp.dot(probs, vb, preferred_element_type=F32).astype(BF16)


def attention(own_lens, q_rot, k_new, v_new, k_loc, v_loc, seqs=8):
    batch, cache_len, head_dim = k_loc.shape
    steps = k_new.shape[1]
    queries = q_rot.shape[1]

    def spec(rows):
        return pl.BlockSpec((seqs, rows, head_dim), lambda i, lens: (i, 0, 0))

    return pl.pallas_call(
        functools.partial(attention_kernel, seqs, steps, queries // steps),
        grid_spec=pltpu.PrefetchScalarGridSpec(
            num_scalar_prefetch=1,
            grid=(batch // seqs,),
            in_specs=[spec(queries), spec(steps), spec(steps), spec(cache_len), spec(cache_len)],
            out_specs=[spec(queries), spec(cache_len), spec(cache_len)],
        ),
        out_shape=[
            jax.ShapeDtypeStruct(q_rot.shape, BF16),
            jax.ShapeDtypeStruct(k_loc.shape, BF16),
            jax.ShapeDtypeStruct(v_loc.shape, BF16),
        ],
        compiler_params=pltpu.CompilerParams(vmem_limit_bytes=40 * MIB),
        name="attention_rows",
    )(own_lens, q_rot, k_new, v_new, k_loc, v_loc)


def head_kernel(tile, sub, scale, z_ref, next_ref, e_ref, m_ref, s_ref, t_ref):
    step = pl.program_id(0)
    rows = z_ref.shape[0]

    @pl.when(step == 0)
    def _():
        m_ref[...] = jnp.full_like(m_ref, -jnp.inf)
        s_ref[...] = jnp.zeros_like(s_ref)
        t_ref[...] = jnp.zeros_like(t_ref)

    top, acc, hit = m_ref[...], s_ref[...], t_ref[...]
    wanted = next_ref[...] - step * tile - lax.broadcasted_iota(jnp.int32, (8, rows), 0)
    for part in range(tile // sub):
        dots = lax.dot_general(
            e_ref[part * sub:(part + 1) * sub, :], z_ref[...], (((1,), (1,)), ((), ())), preferred_element_type=F32)
        dots = dots.reshape(sub // 8, 8, rows)
        new_top = jnp.maximum(top, jnp.max(dots, axis=0))
        acc = acc * jnp.exp2((top - new_top) * (scale * LOG2E)) + jnp.sum(
            jnp.exp2((dots - new_top[None]) * (scale * LOG2E)), axis=0)
        top = new_top
        for row in range(sub // 8):
            hit = hit + jnp.where(wanted == part * sub + row * 8, dots[row], 0.0)
    m_ref[...] = top
    s_ref[...] = acc
    t_ref[...] = hit


def head(z_rows, local_next, embed_loc, tile=1280, sub=256):
    rows, width = z_rows.shape
    vocab_dev = embed_loc.shape[0]
    stat = jax.ShapeDtypeStruct((8, rows), F32)
    whole = pl.BlockSpec((8, rows), lambda i: (0, 0))
    return pl.pallas_call(
        functools.partial(head_kernel, tile, sub, width ** -0.5),
        grid=(vocab_dev // tile,),
        in_specs=[
            pl.BlockSpec((rows, width), lambda i: (0, 0)),
            whole,
            pl.BlockSpec((tile, width), lambda i: (i, 0)),
        ],
        out_specs=[whole] * 3,
        out_shape=[stat] * 3,
        compiler_params=pltpu.CompilerParams(vmem_limit_bytes=60 * MIB),
        name="head_rows",
    )(z_rows, jnp.broadcast_to(local_next, (8, rows)), embed_loc)


def solution(mesh):
    group_size = mesh.shape['tp']

    def device_fn(tok_ids, next_ids, seq_lens, embed_loc, ln_gain, w_in_loc, w_out_loc, final_gain, k_loc, v_loc):
        num_steps, batch_size = tok_ids.shape
        batch_dev = batch_size // group_size
        vocab_dev, model_dim = embed_loc.shape
        cache_len, head_dim = k_loc.shape[1:]
        in_dev = w_in_loc.shape[1]
        out_dev = w_out_loc.shape[0]
        kv_dev = 2 * head_dim // group_size
        attn_dev = 2 * out_dev - in_dev + kv_dev
        ff_dev = out_dev - attn_dev
        qkv_dev = attn_dev + kv_dev
        attn_width = attn_dev * group_size
        num_heads = attn_width // head_dim
        own_rows = num_steps * batch_dev
        scale = model_dim ** -0.5
        dev_index = lax.axis_index('tp')
        vocab_start = dev_index * vocab_dev
        own_lens = lax.dynamic_slice_in_dim(seq_lens, dev_index * batch_dev, batch_dev)

        def to_rows(ids):
            return ids.reshape(num_steps, group_size, batch_dev).transpose(1, 0, 2).reshape(-1)

        x_part = gather_rows(to_rows(tok_ids) - vocab_start, embed_loc)
        normed, x_own = exchange(x_part, None, ln_gain, 0)
        proj_out = jnp.dot(normed, w_in_loc, preferred_element_type=F32).astype(BF16)
        gate_proj = proj_out[:, qkv_dev:qkv_dev + ff_dev].astype(F32)
        up_proj = proj_out[:, qkv_dev + ff_dev:].astype(F32)
        mlp_act = (jax.nn.silu(gate_proj) * up_proj).astype(BF16)
        qkv_own = lax.all_to_all(proj_out[:, :qkv_dev], 'tp', 0, 1, tiled=True)
        positions = (own_lens[None, :] + jnp.arange(num_steps)[:, None]).reshape(-1)
        half = head_dim // 2
        inv_freq = ROPE_BASE ** (-jnp.arange(half, dtype=F32) / half)
        angles = positions.astype(F32)[:, None] * inv_freq
        cosine = jnp.cos(angles)[:, None, :]
        sine = jnp.sin(angles)[:, None, :]
        qk = qkv_own[:, :attn_width + head_dim].reshape(own_rows, num_heads + 1, head_dim).astype(F32)
        lo, hi = qk[..., :half], qk[..., half:]
        rot = jnp.concatenate([lo * cosine - hi * sine, hi * cosine + lo * sine], axis=-1)

        def by_seq(rows):
            return rows.reshape(num_steps, batch_dev, -1, head_dim).transpose(1, 0, 2, 3).reshape(batch_dev, -1, head_dim)

        q_rot = by_seq((rot[:, :num_heads] * head_dim ** -0.5).astype(BF16))
        k_new = by_seq(rot[:, num_heads:].astype(BF16))
        v_new = by_seq(qkv_own[:, attn_width + head_dim:])
        attn_out, k_out, v_out = attention(own_lens, q_rot, k_new, v_new, k_loc, v_loc)
        attn_out = attn_out.reshape(batch_dev, num_steps, attn_width).transpose(1, 0, 2).reshape(own_rows, attn_width)
        attn_cols = lax.all_to_all(attn_out, 'tp', 1, 0, tiled=True)
        combined = jnp.concatenate([attn_cols, mlp_act], axis=1)
        part_out = jnp.dot(combined, w_out_loc, preferred_element_type=F32).astype(BF16)
        z_rows, _ = exchange(part_out, x_own, final_gain, 1)
        top, acc, hit = head(z_rows, to_rows(next_ids) - vocab_start, embed_loc)
        row_top = jnp.max(top, axis=0)
        row_acc = jnp.sum(acc * jnp.exp2((top - row_top) * (scale * LOG2E)), axis=0)
        row_hit = jnp.sum(hit, axis=0)
        stats = lax.all_gather(jnp.stack([row_top, row_acc, row_hit]), 'tp')
        all_top = jnp.max(stats[:, 0], axis=0)
        all_acc = jnp.sum(stats[:, 1] * jnp.exp2((stats[:, 0] - all_top) * (scale * LOG2E)), axis=0)
        target = jnp.sum(stats[:, 2], axis=0)
        logp = (target - all_top) * scale - jnp.log(all_acc)
        logp = logp.reshape(group_size, num_steps, batch_dev).transpose(1, 0, 2).reshape(num_steps, batch_size)
        return logp, k_out, v_out

    cache_spec = P('tp', None, None)
    return jax.shard_map(device_fn, mesh=mesh, in_specs=(P(), P(), P(), P('tp', None), P(), P(None, 'tp'), P('tp', None), P(), cache_spec, cache_spec), out_specs=(P(), cache_spec, cache_spec), check_vma=False)
```

profile of v0, /device:TPU:0, one launch (start us, length us, event | category | flops | bytes accessed | tf_op | source)
XLA Modules:
  0.0 393.3 jit_solution(2356337279262049319)
XLA Ops:
  0.6 0.7 broadcast_subtract_fusion
  1.3 0.1 sub.58
  1.4 0.7 sub.60.ids_ref
  2.1 0.7 reshape.152.refs_1_
  2.8 12.7 %gather_rows.1 = bf16[1024,2048]{1,0:T(8,128)(2,1)} custom-call(s32[1024]{0:T(1024)} %sub.60.ids_ref, bf16[32000,2048]{1,0:T(8,128)(2,1)} %e_ref.1), custom_call_target="tpu_custom_call" | custom-call | tf_op jit(solution)/shard_map/gather_rows/pallas_call | solution.py:83
  15.5 2.2 copy-done.1
  17.7 54.8 %exchange_rows.2 = (bf16[4,2,128,2048]{3,2,1,0:T(8,128)(2,1)S(1)}, bf16[128,2048]{1,0:T(8,128)(2,1)S(1)}) custom-call(bf16[4,2,128,2048]{3,2,1,0:T(8,128)(2,1)S(1)} %bitcast.71, bf16[1,2048]{1,0:T(2,128)(2,1)S(1)} %reshape.152.refs_1_), custom_call_target="tpu_custom_call" | custom-call | tf_op jit(solution)/shard_map/exchange_rows/pallas_call | solution.py:191
  72.5 21.9 %convolution_convert_fusion = bf16[1024,4416]{0,1:T(8,128)(2,1)S(1)} fusion(bf16[1024,2048]{1,0:T(8,128)(2,1)S(1)} %bitcast.76, bf16[2048,4416]{0,1:T(8,128)(2,1)} %param.15), kind=kOutput, calls=%fused_computation.2 | convolution fusion | flops 18526568448 | bytes 31326208 | tf_op jit(solution)/shard_map/dot_general | solution.py:335
  94.4 3.5 copy-done.4
  97.9 1.0 copy_bitcast_fusion
  98.8 2.3 all-to-all-start
  101.1 0.8 dynamic_slice.3.lens_ref
  101.9 0.1 convert_element_type.39
  102.0 0.3 multiply_cosine_fusion
  102.3 9.9 %all-to-all-done = bf16[8,128,320]{1,2,0:T(8,128)(2,1)S(1)} async-done(((bf16[8,128,320]{1,2,0:T(8,128)(2,1)}), bf16[8,128,320]{1,2,0:T(8,128)(2,1)S(1)}, u32[]{:S(2)}, u32[]{:S(2)}) %all-to-all-start) | async-done | bytes 655392 | tf_op jit(solution)/shard_map/all_to_all | solution.py:339
  112.2 0.1 convert.5
  112.3 0.2 multiply_add_fusion
  112.5 0.1 fusion.14
  112.6 0.4 copy.38
  113.1 0.1 copy.40
  113.2 0.1 copy.79
  113.3 0.1 copy.42
  113.4 0.1 copy.78
  113.5 2.2 copy-done.2
  115.7 2.2 copy-done.3
  117.8 22.4 %attention_rows.1 = (bf16[64,16,256]{2,1,0:T(8,128)(2,1)S(1)}, bf16[64,128,256]{2,1,0:T(8,128)(2,1)}, bf16[64,128,256]{2,1,0:T(8,128)(2,1)}) custom-call(s32[64]{0:T(128)S(1)} %dynamic_slice.3.lens_ref, bf16[64,16,256]{2,1,0:T(8,128)(2,1)S(1)} %bitcast.73, bf16[64,2,256]{2,1,0:T(2,128)(2,1)S(1)} %bitcast.74, bf16[64,2,256]{2,1,0:T(2,128)(2,1)S(1)} %bitcast.75, ...), custom_call_target="tpu_custom_call" | custom-call | tf_op jit(solution)/shard_map/attention_rows/pallas_call | solution.py:243
  140.2 0.1 reshape.160
  140.4 0.2 copy.44
  140.5 0.1 copy.56
  140.7 0.9 copy.45
  141.6 2.4 all-to-all-start.1
  144.0 6.2 %fusion.4 = bf16[1024,2048]{0,1:T(8,128)(2,1)} fusion(bf16[1024,4416]{0,1:T(8,128)(2,1)} %copy-done.4), kind=kLoop, calls=%fused_computation.7 | loop fusion | flops 16777216 | bytes 12582912 | tf_op jit(solution)/shard_map/convert_element_type | solution.py:338
  150.2 0.1 sub.63
  150.3 0.1 sub.65
  150.4 3.0 all-to-all-done.1
  153.4 0.2 copy.51
  153.6 14.0 %fusion.9 = bf16[1024,2048]{1,0:T(8,128)(2,1)S(1)} fusion(bf16[2304,2048]{1,0:T(8,128)(2,1)} %param.16, bf16[1024,2048]{0,1:T(8,128)(2,1)} %fusion.4, bf16[1024,256]{0,1:T(8,128)(2,1)S(1)} %copy.51), kind=kOutput, calls=%fused_computation.12 | convolution fusion | flops 9675210752 | bytes 18350080 | tf_op jit(solution)/shard_map/dot_general | solution.py:360
  167.6 51.4 %exchange_rows.3 = bf16[4,2,128,2048]{3,2,1,0:T(8,128)(2,1)S(1)} custom-call(bf16[4,2,128,2048]{3,2,1,0:T(8,128)(2,1)S(1)} %bitcast.72, bf16[128,2048]{1,0:T(8,128)(2,1)S(1)} %get-tuple-element.13.refs_1_, bf16[1,2048]{1,0:T(2,128)(2,1)S(1)} %reshape.162.refs_2_), custom_call_target="tpu_custom_call" | custom-call | tf_op jit(solution)/shard_map/exchange_rows/pallas_call | solution.py:191
  219.0 1.9 copy-done
  220.9 0.6 broadcast_in_dim.2.next_ref
  221.5 157.4 %head_rows.1 = (f32[8,1024]{1,0:T(8,128)}, f32[8,1024]{1,0:T(8,128)}, f32[8,1024]{1,0:T(8,128)}) custom-call(bf16[1024,2048]{1,0:T(8,128)(2,1)} %bitcast.70, s32[8,1024]{1,0:T(8,128)} %broadcast_in_dim.2.next_ref, bf16[32000,2048]{1,0:T(8,128)(2,1)} %e_ref.1), custom_call_target="tpu_custom_call" | custom-call | tf_op jit(solution)/shard_map/head_rows/pallas_call | solution.py:293
  378.9 0.8 reduce_sum.37
  379.7 0.8 reduce_max.18
  380.5 0.8 multiply_reduce_fusion
  381.3 11.1 %all-gather.1 = f32[8,3,1024]{2,1,0:T(4,128)S(1)} all-gather(f32[1,3,1024]{2,1,0:T(4,128)S(1)} %maximum_bitcast_fusion), channel_id=2, replica_groups=mesh['tp'=8] {'tp'}, dimensions={0}, use_global_device_ids=true | all-gather | bytes 110592 | tf_op jit(solution)/shard_map/all_gather | solution.py:366
  392.4 0.1 slice_reduce_fusion
  392.6 0.1 sub.72
  392.6 0.7 reshape.164
  (20 shorter events, 0.2 us)
Async XLA Ops:
  15.5 2.2 copy-start.1
  94.4 3.5 copy-start.4
  98.8 13.3 %all-to-all-start = ((bf16[8,128,320]{1,2,0:T(8,128)(2,1)}), bf16[8,128,320]{1,2,0:T(8,128)(2,1)S(1)}, u32[]{:S(2)}, u32[]{:S(2)}) async-start(bf16[8,128,320]{1,2,0:T(8,128)(2,1)} %copy_bitcast_fusion), calls=%async_computation | async-start | bytes 1310720 | tf_op jit(solution)/shard_map/all_to_all | solution.py:339
  113.5 2.2 copy-start.2
  115.7 2.2 copy-start.3
  140.4 9.9 %copy-start.5 = (bf16[2048]{0:T(1024)(128)(2,1)S(1)}, bf16[2048]{0:T(1024)(128)(2,1)}, u32[]{:S(2)}) copy-start(bf16[2048]{0:T(1024)(128)(2,1)} %param.17) | copy-start | bytes 12292
  141.6 11.8 %all-to-all-start.1 = ((bf16[128,8,256]{2,0,1:T(8,128)(2,1)}), bf16[128,8,256]{2,0,1:T(8,128)(2,1)S(1)}, u32[]{:S(2)}, u32[]{:S(2)}) async-start(bf16[128,8,256]{2,0,1:T(8,128)(2,1)} %copy.45), calls=%async_computation.1 | async-start | bytes 1048576 | tf_op jit(solution)/shard_map/all_to_all | solution.py:358
  219.0 1.9 copy-start
where the time goes:
time: 394 us; the launch traced here: 393 us
  Pallas kernels  299 us (76%)
  matrix products  35.9 us (9%)
  local copies, waits for them, and re-layouts  19.1 us (5%)
  waiting for transfers between devices  12.9 us (3%)
  blocking collectives  11.1 us (3%)
  other arithmetic  10.1 us (3%)
  starting transfers between devices  4.68 us (1%)
    pallas_call x1, Pallas kernels, head(): pl.pallas_call(functools.partial(head_kernel, tile, sub, width ** (-0.5))...  157 us
    pallas_call x2, Pallas kernels, exchange(): pl.pallas_call(functools.partial(exchange_kernel, chunks, with_base), in_...  106 us
    pallas_call x1, Pallas kernels, attention(): pl.pallas_call(functools.partial(attention_kernel, seqs, steps, queries /...  22.4 us
    dot_general x1, matrix products, device_fn(): jnp.dot(normed, w_in_loc, preferred_element_type=F32).astype(BF16)  21.9 us
    dot_general x1, matrix products, device_fn(): jnp.dot(combined, w_out_loc, preferred_element_type=F32).astype(BF16)  14 us
    pallas_call x1, Pallas kernels, gather_rows(): pl.pallas_call(functools.partial(gather_kernel, count, vocab_dev), grid_s...  12.7 us
    unnamed x13, local copies, waits for them, and re-layouts  12.1 us
    all_gather x1, blocking collectives, device_fn(): stats = lax.all_gather(jnp.stack([row_top, row_acc, row_hit]), 'tp')  11.1 us
  transfers between devices with their start and end apart: 2, of which 2 were waited for; matrix products, arithmetic and copies ran while one was open for 2% of the time, Pallas kernels for 0%

commit v1 on v0

v1 whole, which is shorter than its diff:
```python
import functools
import math

import jax
import jax.numpy as jnp
from jax import lax
from jax.experimental import pallas as pl
from jax.experimental.pallas import tpu as pltpu
from jax.sharding import PartitionSpec as P

ROPE_BASE = 10000.0
NORM_EPS = 1e-6
LOG2E = 1.4426950408889634
MESH_ID = pl.DeviceIdType.MESH
F32 = jnp.float32
BF16 = jnp.bfloat16
MIB = 2 ** 20


def norm_rows(values, gain_row):
    centered = values - jnp.mean(values, axis=-1, keepdims=True)
    variance = jnp.mean(jnp.square(centered), axis=-1, keepdims=True)
    return (centered * lax.rsqrt(variance + NORM_EPS) * gain_row.astype(F32)).astype(BF16)


def gather_kernel(count, vocab_dev, ids_ref, embed_ref, out_ref, blocks, rows, wide, slots, sem):
    width = out_ref.shape[1]
    per_loop = 8

    def compact(idx, total):
        for sub in range(per_loop):
            pos = idx * per_loop + sub
            local_id = ids_ref[pos]
            slots[total] = pos
            total = total + jnp.where((local_id >= 0) & (local_id < vocab_dev), 1, 0)
        return total

    total = lax.fori_loop(0, count // per_loop, compact, jnp.int32(0))

    def block_copy(slot):
        local_id = ids_ref[slots[slot]]
        start = pl.multiple_of((local_id // 8) * 8, 8)
        return pltpu.make_async_copy(embed_ref.at[pl.ds(start, 8), :], blocks.at[slot], sem)

    def issue(slot, carry):
        block_copy(slot).start()
        return carry

    lax.fori_loop(0, total, issue, 0)
    rows[...] = jnp.zeros_like(rows)

    def drain(slot, carry):
        pltpu.make_async_copy(embed_ref.at[pl.ds(0, 8), :], blocks.at[slot], sem).wait()
        return carry

    lax.fori_loop(0, total, drain, 0)

    def pick(idx, carry):
        for sub in range(4):
            slot = idx * 4 + sub

            @pl.when(slot < total)
            def _():
                wide[sub] = blocks[slot].astype(F32)

        for sub in range(4):
            slot = idx * 4 + sub

            @pl.when(slot < total)
            def _():
                pos = slots[slot]
                rows[pl.ds(pos, 1), :] = wide[sub, pl.ds(lax.rem(ids_ref[pos], 8), 1), :]

        return carry

    lax.fori_loop(0, (total + 3) // 4, pick, 0)
    out_ref[...] = rows[...].astype(BF16)


def gather_rows(local_ids, embed_loc):
    count = local_ids.shape[0]
    vocab_dev, width = embed_loc.shape
    return pl.pallas_call(
        functools.partial(gather_kernel, count, vocab_dev),
        grid_spec=pltpu.PrefetchScalarGridSpec(
            num_scalar_prefetch=1,
            grid=(1,),
            in_specs=[pl.BlockSpec(memory_space=pl.ANY)],
            out_specs=pl.BlockSpec((count, width), lambda i, ids: (0, 0)),
            scratch_shapes=[
                pltpu.VMEM((count, 8, width), BF16),
                pltpu.VMEM((count, width), F32),
                pltpu.VMEM((4, 8, width), F32),
                pltpu.SMEM((count + 1,), jnp.int32),
                pltpu.SemaphoreType.DMA,
            ],
        ),
        out_shape=jax.ShapeDtypeStruct((count, width), BF16),
        compiler_params=pltpu.CompilerParams(vmem_limit_bytes=60 * MIB),
        name="gather_rows",
    )(local_ids, embed_loc)


def project_kernel(chunks, qkv_dev, ff_dev, *refs):
    (part, gain, w_ref, own, act, qkv_all, w_buf, full, pair_buf, send_buf, recv_buf, qkv_buf,
     w_sem, pair_sems, sum_sems, own_sems, all_sems, fwd_sems, qkv_sems) = refs
    me = lax.axis_index("tp")
    chip, core = me // 2, lax.rem(me, 2)
    other = 1 - core
    mate = chip * 2 + other
    chips = [chip, lax.rem(chip, 2) * (-2) + chip + 1, lax.rem(chip + 2, 4), 3 - chip]
    peers = [chips[k] * 2 + core for k in range(4)]
    others = [lax.rem(me + k, 8) for k in range(1, 8)]
    width = part.shape[3]
    size = part.shape[2] // chunks
    count = 8 * size

    w_copy = pltpu.make_async_copy(w_ref, w_buf, w_sem)
    w_copy.start()
    barrier = pltpu.get_barrier_semaphore()
    for target in others:
        pl.semaphore_signal(barrier, inc=1, device_id=(target,), device_id_type=MESH_ID)
    pl.semaphore_wait(barrier, 7)

    def span(c):
        return pl.ds(c * size, size)

    def remote(src, dst, sems, idx, target):
        return pltpu.make_async_remote_copy(
            src_ref=src, dst_ref=dst, send_sem=sems.at[(0,) + idx], recv_sem=sems.at[(1,) + idx],
            device_id=(target,), device_id_type=MESH_ID)

    def pair_copy(c):
        return remote(part.at[:, other, span(c), :], pair_buf.at[:, span(c), :], pair_sems, (c,), mate)

    def sum_copy(k, c):
        return remote(send_buf.at[k - 1, span(c), :], recv_buf.at[k - 1, span(c), :], sum_sems, (k - 1, c), peers[k])

    def all_copy(k, c):
        mine = full.at[c, chip, core]
        if k == 0:
            return remote(mine, mine, own_sems, (c,), mate)
        return remote(mine, mine, all_sems, (k - 1, c), peers[k])

    def fwd_copy(k, c):
        there = full.at[c, chips[k], core]
        return remote(there, there, fwd_sems, (k - 1, c), mate)

    def qkv_copy(k, c):
        return remote(qkv_buf.at[c, others[k]], qkv_all.at[me, span(c), :], qkv_sems, (k, c), others[k])

    def send_sums(c):
        pair_copy(c).wait_recv()
        for k in (3, 1, 2):
            both = part[chips[k], core, span(c), :].astype(F32) + pair_buf[chips[k], span(c), :].astype(F32)
            send_buf[k - 1, span(c), :] = both.astype(BF16)
            sum_copy(k, c).start()

    def send_rows(c):
        total = part[chip, core, span(c), :].astype(F32) + pair_buf[chip, span(c), :].astype(F32)
        for k in (1, 2, 3):
            sum_copy(k, c).wait_recv()
            total = total + recv_buf[k - 1, span(c), :].astype(F32)
        summed = total.astype(BF16)
        own[span(c), :] = summed
        full[c, chip, core] = norm_rows(summed.astype(F32), gain[...])
        for k in (3, 1, 2, 0):
            all_copy(k, c).start()

    def forward_rows(c):
        for k in (1, 2, 3):
            all_copy(k, c).wait_recv()
            fwd_copy(k, c).start()

    def project(c):
        all_copy(0, c).wait_recv()
        for k in (1, 2, 3):
            fwd_copy(k, c).wait_recv()
        if c == 0:
            w_copy.wait()
        rows = full[c].reshape(count, width)
        def columns(start, count):
            return lax.dot_general(
                rows, w_buf[pl.ds(start, count), :], (((1,), (1,)), ((), ())), preferred_element_type=F32).astype(BF16)

        qkv_buf[c] = columns(0, qkv_dev).reshape(8, size, qkv_dev)
        qkv_all[me, span(c), :] = qkv_buf[c, me]
        for k in range(7):
            qkv_copy(k, c).start()

        def mlp_tile(t, carry):
            at = pl.multiple_of(t * 256, 256)
            gate = columns(pl.multiple_of(qkv_dev + at, 64), 256).astype(F32)
            up = columns(pl.multiple_of(qkv_dev + ff_dev + at, 64), 256).astype(F32)
            act[:, span(c), pl.ds(at, 256)] = (jax.nn.silu(gate) * up).astype(BF16).reshape(8, size, 256)
            return carry

        lax.fori_loop(0, ff_dev // 256, mlp_tile, 0)

    for c in range(chunks):
        pair_copy(c).start()
    send_sums(0)
    send_sums(1)
    send_rows(0)
    send_sums(2)
    send_rows(1)
    send_sums(3)
    forward_rows(0)
    project(0)
    send_rows(2)
    forward_rows(1)
    project(1)
    send_rows(3)
    forward_rows(2)
    project(2)
    forward_rows(3)
    project(3)
    for c in range(chunks):
        for k in range(7):
            qkv_copy(k, c).wait_recv()
    for c in range(chunks):
        pair_copy(c).wait_send()
        all_copy(0, c).wait_send()
        for k in (1, 2, 3):
            sum_copy(k, c).wait_send()
            all_copy(k, c).wait_send()
            fwd_copy(k, c).wait_send()
        for k in range(7):
            qkv_copy(k, c).wait_send()


def project(part, gain, w_in_loc, qkv_dev, ff_dev, cid, chunks=4):
    rows, width = part.shape
    own_rows = rows // 8
    size = own_rows // chunks
    vmem = pl.BlockSpec(memory_space=pltpu.VMEM)
    dma = pltpu.SemaphoreType.DMA
    return pl.pallas_call(
        functools.partial(project_kernel, chunks, qkv_dev, ff_dev),
        in_specs=[vmem, vmem, pl.BlockSpec(memory_space=pl.ANY)],
        out_specs=[vmem] * 3,
        out_shape=[
            jax.ShapeDtypeStruct((own_rows, width), BF16),
            jax.ShapeDtypeStruct((8, own_rows, ff_dev), BF16),
            jax.ShapeDtypeStruct((8, own_rows, qkv_dev), BF16),
        ],
        scratch_shapes=[
            pltpu.VMEM(w_in_loc.shape[::-1], BF16),
            pltpu.VMEM((chunks, 4, 2, size, width), BF16),
            pltpu.VMEM((4, own_rows, width), BF16),
            pltpu.VMEM((3, own_rows, width), BF16),
            pltpu.VMEM((3, own_rows, width), BF16),
            pltpu.VMEM((chunks, 8, size, qkv_dev), BF16),
            dma, dma((2, chunks)), dma((2, 3, chunks)), dma((2, chunks)), dma((2, 3, chunks)), dma((2, 3, chunks)),
            dma((2, 7, chunks)),
        ],
        compiler_params=pltpu.CompilerParams(collective_id=cid, has_side_effects=True, vmem_limit_bytes=60 * MIB),
        name="project_rows",
    )(part.reshape(4, 2, own_rows, width), gain.reshape(1, width), w_in_loc.T)


def attention_kernel(seqs, steps, heads, lens_ref, q_ref, kn_ref, vn_ref, k_ref, v_ref, o_ref, ko_ref, vo_ref):
    first = pl.program_id(0) * seqs
    cache_len = k_ref.shape[1]
    head_dim = k_ref.shape[2]
    times = lax.broadcasted_iota(jnp.int32, (cache_len, head_dim), 0)
    qtime = lax.broadcasted_iota(jnp.int32, (steps * heads, cache_len), 1)
    qstep = lax.broadcasted_iota(jnp.int32, (steps * heads, cache_len), 0) // heads
    scores = []
    values = []
    for b in range(seqs):
        pos = lens_ref[first + b]
        kb = k_ref[b].astype(F32)
        vb = v_ref[b].astype(F32)
        for s in range(steps):
            hit = times == pos + s
            kb = jnp.where(hit, kn_ref[b, s:s + 1, :].astype(F32), kb)
            vb = jnp.where(hit, vn_ref[b, s:s + 1, :].astype(F32), vb)
        kb = kb.astype(BF16)
        vb = vb.astype(BF16)
        ko_ref[b] = kb
        vo_ref[b] = vb
        dots = lax.dot_general(q_ref[b], kb, (((1,), (1,)), ((), ())), preferred_element_type=F32)
        scores.append(jnp.where(qtime <= pos + qstep, dots, -jnp.inf))
        values.append(vb)
    scores = jnp.concatenate(scores, axis=0)
    expd = jnp.exp(scores - jnp.max(scores, axis=-1, keepdims=True))
    probs = (expd / jnp.sum(expd, axis=-1, keepdims=True)).astype(BF16)
    queries = steps * heads
    for b in range(seqs):
        o_ref[b] = jnp.dot(probs[b * queries:(b + 1) * queries], values[b], preferred_element_type=F32).astype(BF16)


def attention(own_lens, q_rot, k_new, v_new, k_loc, v_loc, seqs=8):
    batch, cache_len, head_dim = k_loc.shape
    steps = k_new.shape[1]
    queries = q_rot.shape[1]

    def spec(rows):
        return pl.BlockSpec((seqs, rows, head_dim), lambda i, lens: (i, 0, 0))

    return pl.pallas_call(
        functools.partial(attention_kernel, seqs, steps, queries // steps),
        grid_spec=pltpu.PrefetchScalarGridSpec(
            num_scalar_prefetch=1,
            grid=(batch // seqs,),
            in_specs=[spec(queries), spec(steps), spec(steps), spec(cache_len), spec(cache_len)],
            out_specs=[spec(queries), spec(cache_len), spec(cache_len)],
        ),
        out_shape=[
            jax.ShapeDtypeStruct(q_rot.shape, BF16),
            jax.ShapeDtypeStruct(k_loc.shape, BF16),
            jax.ShapeDtypeStruct(v_loc.shape, BF16),
        ],
        compiler_params=pltpu.CompilerParams(vmem_limit_bytes=40 * MIB),
        name="attention_rows",
    )(own_lens, q_rot, k_new, v_new, k_loc, v_loc)


def head_kernel(sizes, tiles, subs, when, scale, *refs):
    (part, base, gain, next_a, next_b, e_ref, out_ref, full_a, full_b, pair_buf, send_buf, recv_buf, tops_a, tops_b,
     stat, stat_all, pair_sems, sum_sems, own_sems, all_sems, fwd_sems, stat_sems) = refs
    step = pl.program_id(0)
    me = lax.axis_index("tp")
    chip, core = me // 2, lax.rem(me, 2)
    other = 1 - core
    mate = chip * 2 + other
    chips = [chip, lax.rem(chip, 2) * (-2) + chip + 1, lax.rem(chip + 2, 4), 3 - chip]
    peers = [chips[k] * 2 + core for k in range(4)]
    others = [lax.rem(me + k, 8) for k in range(1, 8)]
    offsets = (0, sizes[0])
    fulls = (full_a, full_b)
    width = part.shape[3]

    def span(g):
        return pl.ds(offsets[g], sizes[g])

    def remote(src, dst, sems, idx, target):
        return pltpu.make_async_remote_copy(
            src_ref=src, dst_ref=dst, send_sem=sems.at[(0,) + idx], recv_sem=sems.at[(1,) + idx],
            device_id=(target,), device_id_type=MESH_ID)

    def pair_copy(g):
        return remote(part.at[:, other, span(g), :], pair_buf.at[:, span(g), :], pair_sems, (g,), mate)

    def sum_copy(k, g):
        return remote(send_buf.at[k - 1, span(g), :], recv_buf.at[k - 1, span(g), :], sum_sems, (k - 1, g), peers[k])

    def all_copy(k, g):
        mine = fulls[g].at[chip, core]
        if k == 0:
            return remote(mine, mine, own_sems, (g,), mate)
        return remote(mine, mine, all_sems, (k - 1, g), peers[k])

    def fwd_copy(k, g):
        there = fulls[g].at[chips[k], core]
        return remote(there, there, fwd_sems, (k - 1, g), mate)

    def stat_copy(k):
        return remote(stat, stat_all.at[me], stat_sems, (k,), others[k])

    def send_sums(g):
        pair_copy(g).wait_recv()
        for k in (3, 1, 2):
            both = part[chips[k], core, span(g), :].astype(F32) + pair_buf[chips[k], span(g), :].astype(F32)
            send_buf[k - 1, span(g), :] = both.astype(BF16)
            sum_copy(k, g).start()

    def send_rows(g):
        total = part[chip, core, span(g), :].astype(F32) + pair_buf[chip, span(g), :].astype(F32)
        for k in (1, 2, 3):
            sum_copy(k, g).wait_recv()
            total = total + recv_buf[k - 1, span(g), :].astype(F32)
        rows = base[span(g), :].astype(F32) + total.astype(BF16).astype(F32)
        fulls[g][chip, core] = norm_rows(rows, gain[...])
        for k in (3, 1, 2, 0):
            all_copy(k, g).start()

    def forward_rows(g):
        for k in (1, 2, 3):
            all_copy(k, g).wait_recv()
            fwd_copy(k, g).start()

    def rows_here(g):
        all_copy(0, g).wait_recv()
        for k in (1, 2, 3):
            fwd_copy(k, g).wait_recv()

    def logits(g, local_step, next_ref, tops):
        count = 8 * sizes[g]
        tile, sub = tiles[g], subs[g]
        z_rows = fulls[g][...].reshape(count, width)

        @pl.when(local_step == 0)
        def _():
            tops[0] = jnp.full_like(tops[0], -jnp.inf)
            tops[1] = jnp.zeros_like(tops[1])
            tops[2] = jnp.zeros_like(tops[2])

        top, acc, hit = tops[0], tops[1], tops[2]
        wanted = next_ref[...] - local_step * tile - lax.broadcasted_iota(jnp.int32, (8, count), 0)
        for idx in range(tile // sub):
            dots = lax.dot_general(
                e_ref[idx * sub:(idx + 1) * sub, :], z_rows, (((1,), (1,)), ((), ())), preferred_element_type=F32)
            dots = dots.reshape(sub // 8, 8, count)
            new_top = jnp.maximum(top, jnp.max(dots, axis=0))
            acc = acc * jnp.exp2((top - new_top) * (scale * LOG2E)) + jnp.sum(
                jnp.exp2((dots - new_top[None]) * (scale * LOG2E)), axis=0)
            top = new_top
            for row in range(sub // 8):
                hit = hit + jnp.where(wanted == idx * sub + row * 8, dots[row], 0.0)
        tops[0] = top
        tops[1] = acc
        tops[2] = hit

    steps_a = when[0]
    last = pl.num_programs(0) - 1

    @pl.when(step == 0)
    def _():
        barrier = pltpu.get_barrier_semaphore()
        for target in others:
            pl.semaphore_signal(barrier, inc=1, device_id=(target,), device_id_type=MESH_ID)
        pl.semaphore_wait(barrier, 7)
        pair_copy(0).start()
        pair_copy(1).start()
        send_sums(0)
        send_rows(0)
        send_sums(1)
        forward_rows(0)
        rows_here(0)

    @pl.when(step == when[1])
    def _():
        send_rows(1)

    @pl.when(step == when[2])
    def _():
        forward_rows(1)

    @pl.when(step < steps_a)
    def _():
        logits(0, step, next_a, tops_a)

    @pl.when(step == steps_a)
    def _():
        rows_here(1)

    @pl.when(step >= steps_a)
    def _():
        logits(1, step - steps_a, next_b, tops_b)

    @pl.when(step == last)
    def _():
        for g, tops in ((0, tops_a), (1, tops_b)):
            cols = slice(8 * offsets[g], 8 * (offsets[g] + sizes[g]))
            top = jnp.max(tops[0], axis=0, keepdims=True)
            stat[0:1, cols] = top
            stat[1:2, cols] = jnp.sum(tops[1] * jnp.exp2((tops[0] - top) * (scale * LOG2E)), axis=0, keepdims=True)
            stat[2:3, cols] = jnp.sum(tops[2], axis=0, keepdims=True)
        for k in range(7):
            stat_copy(k).start()
        stat_all[me] = stat[...]
        for k in range(7):
            stat_copy(k).wait_recv()
        top = stat_all[0, 0:1, :]
        for d in range(1, 8):
            top = jnp.maximum(top, stat_all[d, 0:1, :])
        acc = jnp.zeros_like(top)
        hit = jnp.zeros_like(top)
        for d in range(8):
            acc = acc + stat_all[d, 1:2, :] * jnp.exp2((stat_all[d, 0:1, :] - top) * (scale * LOG2E))
            hit = hit + stat_all[d, 2:3, :]
        out_ref[...] = (hit - top) * scale - jnp.log(acc)
        for k in range(7):
            stat_copy(k).wait_send()
        for g in (0, 1):
            pair_copy(g).wait_send()
            all_copy(0, g).wait_send()
            for k in (1, 2, 3):
                sum_copy(k, g).wait_send()
                all_copy(k, g).wait_send()
                fwd_copy(k, g).wait_send()


def head(part, base, gain, local_next, embed_loc, cid, sizes=(32, 96), tiles=(3200, 3200), subs=(640, 640), when=(10, 4, 8)):
    rows, width = part.shape
    own_rows = rows // 8
    vocab_dev = embed_loc.shape[0]
    steps_a, steps_b = vocab_dev // tiles[0], vocab_dev // tiles[1]
    vmem = pl.BlockSpec(memory_space=pltpu.VMEM)
    per_dev = local_next.reshape(8, own_rows)
    wanted = [jnp.broadcast_to(ids.reshape(1, -1), (8, ids.size)) for ids in (per_dev[:, :sizes[0]], per_dev[:, sizes[0]:])]
    dma = pltpu.SemaphoreType.DMA
    out = pl.pallas_call(
        functools.partial(head_kernel, sizes, tiles, subs, (steps_a,) + when[1:], width ** -0.5),
        grid=(steps_a + steps_b,),
        in_specs=[vmem] * 5 + [pl.BlockSpec((tiles[0], width), lambda i: (lax.rem(i, steps_a), 0))],
        out_specs=vmem,
        out_shape=jax.ShapeDtypeStruct((1, rows), F32),
        scratch_shapes=[
            pltpu.VMEM((4, 2, sizes[0], width), BF16),
            pltpu.VMEM((4, 2, sizes[1], width), BF16),
            pltpu.VMEM((4, own_rows, width), BF16),
            pltpu.VMEM((3, own_rows, width), BF16),
            pltpu.VMEM((3, own_rows, width), BF16),
            pltpu.VMEM((3, 8, 8 * sizes[0]), F32),
            pltpu.VMEM((3, 8, 8 * sizes[1]), F32),
            pltpu.VMEM((8, rows), F32),
            pltpu.VMEM((8, 8, rows), F32),
            dma((2, 2)), dma((2, 3, 2)), dma((2, 2)), dma((2, 3, 2)), dma((2, 3, 2)), dma((2, 7)),
        ],
        compiler_params=pltpu.CompilerParams(collective_id=cid, has_side_effects=True, vmem_limit_bytes=63 * MIB),
        name="head_rows",
    )(part.reshape(4, 2, own_rows, width), base, gain.reshape(1, width), *wanted, embed_loc)
    by_a = out[0, :8 * sizes[0]].reshape(8, sizes[0])
    by_b = out[0, 8 * sizes[0]:].reshape(8, sizes[1])
    return jnp.concatenate([by_a, by_b], axis=1)


def solution(mesh):
    group_size = mesh.shape['tp']

    def device_fn(tok_ids, next_ids, seq_lens, embed_loc, ln_gain, w_in_loc, w_out_loc, final_gain, k_loc, v_loc):
        num_steps, batch_size = tok_ids.shape
        batch_dev = batch_size // group_size
        vocab_dev, model_dim = embed_loc.shape
        cache_len, head_dim = k_loc.shape[1:]
        in_dev = w_in_loc.shape[1]
        out_dev = w_out_loc.shape[0]
        kv_dev = 2 * head_dim // group_size
        attn_dev = 2 * out_dev - in_dev + kv_dev
        ff_dev = out_dev - attn_dev
        qkv_dev = attn_dev + kv_dev
        attn_width = attn_dev * group_size
        num_heads = attn_width // head_dim
        own_rows = num_steps * batch_dev
        dev_index = lax.axis_index('tp')
        vocab_start = dev_index * vocab_dev
        own_lens = lax.dynamic_slice_in_dim(seq_lens, dev_index * batch_dev, batch_dev)

        def to_rows(ids):
            return ids.reshape(num_steps, group_size, batch_dev).transpose(1, 0, 2).reshape(-1)

        x_part = gather_rows(to_rows(tok_ids) - vocab_start, embed_loc)
        x_own, mlp_act, qkv_parts = project(x_part, ln_gain, w_in_loc, qkv_dev, ff_dev, 0)
        qkv_own = qkv_parts.transpose(1, 0, 2).reshape(own_rows, group_size * qkv_dev)
        positions = (own_lens[None, :] + jnp.arange(num_steps)[:, None]).reshape(-1)
        half = head_dim // 2
        inv_freq = ROPE_BASE ** (-jnp.arange(half, dtype=F32) / half)
        angles = positions.astype(F32)[:, None] * inv_freq
        cosine = jnp.cos(angles)[:, None, :]
        sine = jnp.sin(angles)[:, None, :]
        qk = qkv_own[:, :attn_width + head_dim].reshape(own_rows, num_heads + 1, head_dim).astype(F32)
        lo, hi = qk[..., :half], qk[..., half:]
        rot = jnp.concatenate([lo * cosine - hi * sine, hi * cosine + lo * sine], axis=-1)

        def by_seq(rows):
            return rows.reshape(num_steps, batch_dev, -1, head_dim).transpose(1, 0, 2, 3).reshape(batch_dev, -1, head_dim)

        q_rot = by_seq((rot[:, :num_heads] * head_dim ** -0.5).astype(BF16))
        k_new = by_seq(rot[:, num_heads:].astype(BF16))
        v_new = by_seq(qkv_own[:, attn_width + head_dim:])
        attn_out, k_out, v_out = attention(own_lens, q_rot, k_new, v_new, k_loc, v_loc)
        attn_out = attn_out.reshape(batch_dev, num_steps, attn_width).transpose(1, 0, 2).reshape(own_rows, attn_width)
        attn_cols = lax.all_to_all(attn_out, 'tp', 1, 0, tiled=True)
        mlp_act = mlp_act.reshape(group_size * own_rows, ff_dev)
        combined = jnp.concatenate([attn_cols, mlp_act], axis=1)
        part_out = jnp.dot(combined, w_out_loc, preferred_element_type=F32).astype(BF16)
        logp = head(part_out, x_own, final_gain, to_rows(next_ids) - vocab_start, embed_loc, 1)
        logp = logp.reshape(group_size, num_steps, batch_dev).transpose(1, 0, 2).reshape(num_steps, batch_size)
        return logp, k_out, v_out

    cache_spec = P('tp', None, None)
    return jax.shard_map(device_fn, mesh=mesh, in_specs=(P(), P(), P(), P('tp', None), P(), P(None, 'tp'), P('tp', None), P(), cache_spec, cache_spec), out_specs=(P(), cache_spec, cache_spec), check_vma=False)
```

time: 394 us -> 330 us (0.84)
  matrix products: 35.9 us -> 15.1 us
  Pallas kernels: 299 us -> 285 us
  blocking collectives: 11.1 us -> 0 us
  other arithmetic: 10.1 us -> 1.45 us
  waiting for transfers between devices: 12.9 us -> 8.39 us
    dot_general x1 -> x0, matrix products: 21.9 us -> none  [device_fn(): jnp.dot(normed, w_in_loc, preferred_element_type=F32).astype(BF16)]
    pallas_call x1, Pallas kernels: 22.4 us -> 7.27 us  [attention(): pl.pallas_call(functools.partial(attention_kernel, seqs, steps, queries /...]
    all_gather x1 -> x0, blocking collectives: 11.1 us -> none  [device_fn(): stats = lax.all_gather(jnp.stack([row_top, row_acc, row_hit]), 'tp')]
    all_to_all x1 -> x0, waiting for transfers between devices: 9.88 us -> none  [device_fn(): qkv_own = lax.all_to_all(proj_out[:, :qkv_dev], 'tp', 0, 1, tiled=True)]
    unnamed x13 -> x7, local copies, waits for them, and re-layouts: 12.1 us -> 4.48 us
    convert_element_type x1 -> x0, other arithmetic: 6.22 us -> none  [device_fn(): mlp_act = (jax.nn.silu(gate_proj) * up_proj).astype(BF16)]
    all_to_all x1, waiting for transfers between devices: 2.99 us -> 8.39 us  [device_fn(): attn_cols = lax.all_to_all(attn_out, 'tp', 1, 0, tiled=True)]
    pallas_call x3 -> x2, Pallas kernels: 264 us -> 265 us  [the longest x1 193 us: head(): pl.pallas_call(functools.partial(head_kernel, sizes, tiles, subs, (steps_...]
  transfers between devices with their start and end apart: 2 -> 1, of which waited for: 2 -> 1; matrix products, arithmetic and copies ran while one was open for 2% -> 0% of each run, Pallas kernels for 0% -> 0%
where the time goes in v1:
time: 330 us; the launch traced here: 329 us
  Pallas kernels  285 us (86%)
  local copies, waits for them, and re-layouts  15.4 us (5%)
  matrix products  15.1 us (5%)
  waiting for transfers between devices  8.39 us (3%)
    pallas_call x1, Pallas kernels, head(): pl.pallas_call(functools.partial(head_kernel, sizes, tiles, subs, (steps_...  193 us
    pallas_call x1, Pallas kernels, project(): pl.pallas_call(functools.partial(project_kernel, chunks, qkv_dev, ff_dev)...  71.8 us
    dot_general x1, matrix products, device_fn(): jnp.dot(combined, w_out_loc, preferred_element_type=F32).astype(BF16)  15.1 us
    pallas_call x1, Pallas kernels, gather_rows(): pl.pallas_call(functools.partial(gather_kernel, count, vocab_dev), grid_s...  13.4 us
    all_to_all x1, waiting for transfers between devices, device_fn(): attn_cols = lax.all_to_all(attn_out, 'tp', 1, 0, tiled=True)  8.39 us
    pallas_call x1, Pallas kernels, attention(): pl.pallas_call(functools.partial(attention_kernel, seqs, steps, queries /...  7.27 us
  transfers between devices with their start and end apart: 1, of which 1 were waited for; matrix products, arithmetic and copies ran while one was open for 0% of the time, Pallas kernels for 0%

profile of v1, /device:TPU:0, one launch (start us, length us, event | category | flops | bytes accessed | tf_op | source)
XLA Modules:
  0.0 328.9 jit_solution(8453653188719995668)
XLA Ops:
  0.7 0.8 dynamic_slice.3.lens_ref
  1.4 0.1 convert_element_type.26
  1.5 0.7 broadcast_subtract_fusion
  2.2 0.1 sub.31
  2.3 0.7 sub.33.ids_ref
  3.0 1.3 reshape.147.refs_1_
  4.3 13.4 %gather_rows.1 = bf16[1024,2048]{1,0:T(8,128)(2,1)} custom-call(s32[1024]{0:T(1024)} %sub.33.ids_ref, bf16[32000,2048]{1,0:T(8,128)(2,1)} %refs_5_.1), custom_call_target="tpu_custom_call" | custom-call | tf_op jit(solution)/shard_map/gather_rows/pallas_call | solution.py:83
  17.7 71.8 %project_rows.1 = (bf16[128,2048]{1,0:T(8,128)(2,1)}, bf16[8,128,2048]{2,1,0:T(8,128)(2,1)}, bf16[8,128,320]{2,1,0:T(8,128)(2,1)}) custom-call(bf16[4,2,128,2048]{3,2,1,0:T(8,128)(2,1)} %bitcast.48, bf16[1,2048]{1,0:T(2,128)(2,1)} %reshape.147.refs_1_, bf16[4416,2048]{1,0:T(8,128)(2,1)} %bitcast.47), custom_call_target="tpu_custom_call" | custom-call | tf_op jit(solution)/shard_map/project_rows/pallas_call | solution.py:238
  89.4 1.5 copy.38
  91.0 0.1 convert.5
  91.1 0.3 multiply_cosine_fusion
  91.4 0.2 multiply_add_fusion
  91.6 0.1 fusion.9
  91.7 0.1 copy.41
  91.8 0.1 copy.58
  91.9 0.4 copy.39
  92.3 0.1 copy.43
  92.4 0.1 copy.57
  92.5 0.0 copy-start
  92.5 2.2 copy-done
  94.7 0.0 copy-start.1
  94.7 2.2 copy-done.1
  96.9 7.3 %attention_rows.1 = (bf16[64,16,256]{2,1,0:T(8,128)(2,1)S(1)}, bf16[64,128,256]{2,1,0:T(8,128)(2,1)}, bf16[64,128,256]{2,1,0:T(8,128)(2,1)}) custom-call(s32[64]{0:T(128)S(1)} %dynamic_slice.3.lens_ref, bf16[64,16,256]{2,1,0:T(8,128)(2,1)S(1)} %bitcast.44, bf16[64,2,256]{2,1,0:T(2,128)(2,1)S(1)} %bitcast.45, bf16[64,2,256]{2,1,0:T(2,128)(2,1)S(1)} %bitcast.46, ...), custom_call_target="tpu_custom_call" | custom-call | tf_op jit(solution)/shard_map/attention_rows/pallas_call | solution.py:302
  104.1 0.0 copy-start.2
  104.2 0.1 reshape.155
  104.3 0.2 copy.45
  104.4 0.1 copy.49
  104.6 0.9 copy.46
  105.5 2.4 all-to-all-start
  107.9 0.1 sub.36
  108.0 0.1 sub.38
  108.1 0.1 slice.38
  108.1 0.1 broadcast_in_dim.10
  108.2 0.1 broadcast_in_dim.8
  108.3 0.0 copy-done.2
  108.3 0.6 reshape.158.refs_2_
  108.9 8.4 %all-to-all-done = bf16[128,8,256]{2,0,1:T(8,128)(2,1)S(1)} async-done(((bf16[128,8,256]{2,0,1:T(8,128)(2,1)}), bf16[128,8,256]{2,0,1:T(8,128)(2,1)S(1)}, u32[]{:S(2)}, u32[]{:S(2)}) %all-to-all-start) | async-done | bytes 524320 | tf_op jit(solution)/shard_map/all_to_all | solution.py:566
  117.3 15.1 %fusion.4 = bf16[1024,2048]{1,0:T(8,128)(2,1)} fusion(bf16[2304,2048]{1,0:T(8,128)(2,1)} %param.16, bf16[1024,2048]{1,0:T(8,128)(2,1)} %bitcast.64, bf16[1024,256]{1,0:T(8,128)(2,1)S(1)} %bitcast.57), kind=kOutput, calls=%fused_computation.4 | convolution fusion | flops 9675210752 | bytes 18350080 | tf_op jit(solution)/shard_map/dot_general | solution.py:569
  132.4 0.6 broadcast_in_dim.11.refs_4_
  133.0 0.6 broadcast_in_dim.9.refs_3_
  133.6 193.0 %head_rows.1 = f32[1,1024]{1,0:T(1,128)} custom-call(bf16[4,2,128,2048]{3,2,1,0:T(8,128)(2,1)} %bitcast.49, bf16[128,2048]{1,0:T(8,128)(2,1)} %get-tuple-element.12.refs_1_, bf16[1,2048]{1,0:T(2,128)(2,1)} %reshape.158.refs_2_, s32[8,256]{1,0:T(8,128)} %broadcast_in_dim.9.refs_3_, s32[8,768]{1,0:T(8,128)} %broadcast_in_dim.11.refs_4_, ...), custom_call_target="tpu_custom_call" | custom-call | tf_op jit(solution)/shard_map/head_rows/pallas_call | solution.py:495
  326.6 0.7 slice_reduce_fusion
  327.3 0.7 slice_reduce_fusion.1
  327.9 0.1 reshape_squeeze.7
  328.0 0.1 reshape_squeeze.6
  328.1 0.1 pad_maximum_fusion.1
  328.2 0.1 reshape.159
  328.2 0.7 reshape.160
  (9 shorter events, 0.1 us)
Async XLA Ops:
  92.5 2.2 copy-start
  94.7 2.2 copy-start.1
  104.1 4.1 %copy-start.2 = (bf16[2048]{0:T(1024)(128)(2,1)S(1)}, bf16[2048]{0:T(1024)(128)(2,1)}, u32[]{:S(2)}) copy-start(bf16[2048]{0:T(1024)(128)(2,1)} %param.17) | copy-start | bytes 12292
  105.5 11.8 %all-to-all-start = ((bf16[128,8,256]{2,0,1:T(8,128)(2,1)}), bf16[128,8,256]{2,0,1:T(8,128)(2,1)S(1)}, u32[]{:S(2)}, u32[]{:S(2)}) async-start(bf16[128,8,256]{2,0,1:T(8,128)(2,1)} %copy.46), calls=%async_computation | async-start | bytes 1048576 | tf_op jit(solution)/shard_map/all_to_all | solution.py:566

commit v2 on v1

--- a/solution.py
+++ b/solution.py
@@ -25,7 +25,8 @@
 
 def gather_kernel(count, vocab_dev, ids_ref, embed_ref, out_ref, blocks, rows, wide, slots, sem):
     width = out_ref.shape[1]
-    per_loop = 8
+    per_loop = 16
+    group = wide.shape[0]
 
     def compact(idx, total):
         for sub in range(per_loop):
@@ -56,24 +57,14 @@
     lax.fori_loop(0, total, drain, 0)
 
     def pick(idx, carry):
-        for sub in range(4):
-            slot = idx * 4 + sub
-
-            @pl.when(slot < total)
-            def _():
-                wide[sub] = blocks[slot].astype(F32)
-
-        for sub in range(4):
-            slot = idx * 4 + sub
-
-            @pl.when(slot < total)
-            def _():
-                pos = slots[slot]
-                rows[pl.ds(pos, 1), :] = wide[sub, pl.ds(lax.rem(ids_ref[pos], 8), 1), :]
-
+        found = [slots[jnp.minimum(idx * group + sub, total - 1)] for sub in range(group)]
+        for sub in range(group):
+            wide[sub] = blocks[jnp.minimum(idx * group + sub, total - 1)].astype(F32)
+        for sub in range(group):
+            rows[pl.ds(found[sub], 1), :] = wide[sub, pl.ds(lax.rem(ids_ref[found[sub]], 8), 1), :]
         return carry
 
-    lax.fori_loop(0, (total + 3) // 4, pick, 0)
+    lax.fori_loop(0, (total + group - 1) // group, pick, 0)
     out_ref[...] = rows[...].astype(BF16)
 
 
@@ -90,7 +81,7 @@
             scratch_shapes=[
                 pltpu.VMEM((count, 8, width), BF16),
                 pltpu.VMEM((count, width), F32),
-                pltpu.VMEM((4, 8, width), F32),
+                pltpu.VMEM((8, 8, width), F32),
                 pltpu.SMEM((count + 1,), jnp.int32),
                 pltpu.SemaphoreType.DMA,
             ],
@@ -102,8 +93,8 @@
 
 
 def project_kernel(chunks, qkv_dev, ff_dev, *refs):
-    (part, gain, w_ref, own, act, qkv_all, w_buf, full, pair_buf, send_buf, recv_buf, qkv_buf,
-     w_sem, pair_sems, sum_sems, own_sems, all_sems, fwd_sems, qkv_sems) = refs
+    (part, gain, w_ref, own, act, qkv_all, w_buf, full, pair_buf, one_send, one_recv, two_send, two_recv, qkv_buf,
+     w_sem, pair_sems, one_sems, two_sems, own_sems, near_sems, far_sems, fwd_sems, qkv_sems) = refs
     me = lax.axis_index("tp")
     chip, core = me // 2, lax.rem(me, 2)
     other = 1 - core
@@ -133,14 +124,28 @@
     def pair_copy(c):
         return remote(part.at[:, other, span(c), :], pair_buf.at[:, span(c), :], pair_sems, (c,), mate)
 
-    def sum_copy(k, c):
-        return remote(send_buf.at[k - 1, span(c), :], recv_buf.at[k - 1, span(c), :], sum_sems, (k - 1, c), peers[k])
-
-    def all_copy(k, c):
+    half_cols = width // 2
+
+    def cols(h):
+        return slice(h * half_cols, (h + 1) * half_cols)
+
+    def one_copy(h, c):
+        return remote(one_send.at[h, :, span(c), :], one_recv.at[h, :, span(c), :], one_sems, (h, c), peers[1 + h])
+
+    def two_copy(h, c):
+        return remote(two_send.at[h, span(c), :], two_recv.at[h, span(c), :], two_sems, (h, c), peers[2 - h])
+
+    def give_copy(c):
         mine = full.at[c, chip, core]
-        if k == 0:
-            return remote(mine, mine, own_sems, (c,), mate)
-        return remote(mine, mine, all_sems, (k - 1, c), peers[k])
+        return remote(mine, mine, own_sems, (c,), mate)
+
+    def near_copy(h, c):
+        mine = full.at[c, chip, core, :, cols(h)]
+        return remote(mine, mine, near_sems, (h, c), peers[2 - h])
+
+    def far_copy(h, j, c):
+        block = full.at[c, chips[0 if j == 0 else 2 - h], core, :, cols(h)]
+        return remote(block, block, far_sems, (h, j, c), peers[1 + h])
 
     def fwd_copy(k, c):
         there = full.at[c, chips[k], core]
@@ -149,31 +154,50 @@
     def qkv_copy(k, c):
         return remote(qkv_buf.at[c, others[k]], qkv_all.at[me, span(c), :], qkv_sems, (k, c), others[k])
 
-    def send_sums(c):
+    def both(k, h, c):
+        mine = part[chips[k], core, span(c), cols(h)].astype(F32)
+        return mine + pair_buf[chips[k], span(c), cols(h)].astype(F32)
+
+    def sums_one(c):
         pair_copy(c).wait_recv()
-        for k in (3, 1, 2):
-            both = part[chips[k], core, span(c), :].astype(F32) + pair_buf[chips[k], span(c), :].astype(F32)
-            send_buf[k - 1, span(c), :] = both.astype(BF16)
-            sum_copy(k, c).start()
+        for h in (0, 1):
+            one_send[h, 0, span(c), :] = both(1 + h, h, c).astype(BF16)
+            one_send[h, 1, span(c), :] = both(3, h, c).astype(BF16)
+            one_copy(h, c).start()
+
+    def sums_two(c):
+        for h in (0, 1):
+            one_copy(h, c).wait_recv()
+            two_send[h, span(c), :] = (both(2 - h, h, c) + one_recv[h, 1, span(c), :].astype(F32)).astype(BF16)
+            two_copy(h, c).start()
 
     def send_rows(c):
-        total = part[chip, core, span(c), :].astype(F32) + pair_buf[chip, span(c), :].astype(F32)
-        for k in (1, 2, 3):
-            sum_copy(k, c).wait_recv()
-            total = total + recv_buf[k - 1, span(c), :].astype(F32)
-        summed = total.astype(BF16)
+        totals = []
+        for h in (0, 1):
+            two_copy(h, c).wait_recv()
+            totals.append(both(0, h, c) + one_recv[h, 0, span(c), :].astype(F32) + two_recv[h, span(c), :].astype(F32))
+        summed = jnp.concatenate(totals, axis=1).astype(BF16)
         own[span(c), :] = summed
         full[c, chip, core] = norm_rows(summed.astype(F32), gain[...])
-        for k in (3, 1, 2, 0):
-            all_copy(k, c).start()
+        for h in (0, 1):
+            near_copy(h, c).start()
+            far_copy(h, 0, c).start()
+        give_copy(c).start()
+
+    def relay_rows(c):
+        for h in (0, 1):
+            near_copy(h, c).wait_recv()
+            far_copy(h, 1, c).start()
 
     def forward_rows(c):
+        for h in (0, 1):
+            for j in (0, 1):
+                far_copy(h, j, c).wait_recv()
         for k in (1, 2, 3):
-            all_copy(k, c).wait_recv()
             fwd_copy(k, c).start()
 
     def project(c):
-        all_copy(0, c).wait_recv()
+        give_copy(c).wait_recv()
         for k in (1, 2, 3):
             fwd_copy(k, c).wait_recv()
         if c == 0:
@@ -199,31 +223,24 @@
 
     for c in range(chunks):
         pair_copy(c).start()
-    send_sums(0)
-    send_sums(1)
-    send_rows(0)
-    send_sums(2)
-    send_rows(1)
-    send_sums(3)
-    forward_rows(0)
-    project(0)
-    send_rows(2)
-    forward_rows(1)
-    project(1)
-    send_rows(3)
-    forward_rows(2)
-    project(2)
-    forward_rows(3)
-    project(3)
+    stages = (sums_one, sums_two, send_rows, relay_rows, forward_rows, project)
+    for turn in range(chunks + len(stages) - 1):
+        for depth in range(len(stages)):
+            if 0 <= turn - depth < chunks:
+                stages[depth](turn - depth)
     for c in range(chunks):
         for k in range(7):
             qkv_copy(k, c).wait_recv()
     for c in range(chunks):
         pair_copy(c).wait_send()
-        all_copy(0, c).wait_send()
+        give_copy(c).wait_send()
+        for h in (0, 1):
+            one_copy(h, c).wait_send()
+            two_copy(h, c).wait_send()
+            near_copy(h, c).wait_send()
+            far_copy(h, 0, c).wait_send()
+            far_copy(h, 1, c).wait_send()
         for k in (1, 2, 3):
-            sum_copy(k, c).wait_send()
-            all_copy(k, c).wait_send()
             fwd_copy(k, c).wait_send()
         for k in range(7):
             qkv_copy(k, c).wait_send()
@@ -248,11 +265,13 @@
             pltpu.VMEM(w_in_loc.shape[::-1], BF16),
             pltpu.VMEM((chunks, 4, 2, size, width), BF16),
             pltpu.VMEM((4, own_rows, width), BF16),
-            pltpu.VMEM((3, own_rows, width), BF16),
-            pltpu.VMEM((3, own_rows, width), BF16),
+            pltpu.VMEM((2, 2, own_rows, width // 2), BF16),
+            pltpu.VMEM((2, 2, own_rows, width // 2), BF16),
+            pltpu.VMEM((2, own_rows, width // 2), BF16),
+            pltpu.VMEM((2, own_rows, width // 2), BF16),
             pltpu.VMEM((chunks, 8, size, qkv_dev), BF16),
-            dma, dma((2, chunks)), dma((2, 3, chunks)), dma((2, chunks)), dma((2, 3, chunks)), dma((2, 3, chunks)),
-            dma((2, 7, chunks)),
+            dma, dma((2, chunks)), dma((2, 2, chunks)), dma((2, 2, chunks)), dma((2, chunks)), dma((2, 2, chunks)),
+            dma((2, 2, 2, chunks)), dma((2, 3, chunks)), dma((2, 7, chunks)),
         ],
         compiler_params=pltpu.CompilerParams(collective_id=cid, has_side_effects=True, vmem_limit_bytes=60 * MIB),
         name="project_rows",
@@ -291,7 +310,7 @@
         o_ref[b] = jnp.dot(probs[b * queries:(b + 1) * queries], values[b], preferred_element_type=F32).astype(BF16)
 
 
-def attention(own_lens, q_rot, k_new, v_new, k_loc, v_loc, seqs=8):
+def attention(own_lens, q_rot, k_new, v_new, k_loc, v_loc, seqs=16):
     batch, cache_len, head_dim = k_loc.shape
     steps = k_new.shape[1]
     queries = q_rot.shape[1]
@@ -312,14 +331,14 @@
             jax.ShapeDtypeStruct(k_loc.shape, BF16),
             jax.ShapeDtypeStruct(v_loc.shape, BF16),
         ],
-        compiler_params=pltpu.CompilerParams(vmem_limit_bytes=40 * MIB),
+        compiler_params=pltpu.CompilerParams(vmem_limit_bytes=63 * MIB),
         name="attention_rows",
     )(own_lens, q_rot, k_new, v_new, k_loc, v_loc)
 
 
 def head_kernel(sizes, tiles, subs, when, scale, *refs):
-    (part, base, gain, next_a, next_b, e_ref, out_ref, full_a, full_b, pair_buf, send_buf, recv_buf, tops_a, tops_b,
-     stat, stat_all, pair_sems, sum_sems, own_sems, all_sems, fwd_sems, stat_sems) = refs
+    (attn, act, base, gain, next_ref, w_ref, e_ref, out_ref, w_buf, attn_all, part, full_a, full_b, pair_buf, send_buf, recv_buf, tops_a, tops_b,
+     stat, stat_all, w_sem, attn_sems, pair_sems, sum_sems, own_sems, all_sems, fwd_sems, stat_sems) = refs
     step = pl.program_id(0)
     me = lax.axis_index("tp")
     chip, core = me // 2, lax.rem(me, 2)
@@ -330,7 +349,7 @@
     others = [lax.rem(me + k, 8) for k in range(1, 8)]
     offsets = (0, sizes[0])
     fulls = (full_a, full_b)
-    width = part.shape[3]
+    width = base.shape[1]
 
     def span(g):
         return pl.ds(offsets[g], sizes[g])
@@ -355,6 +374,26 @@
     def fwd_copy(k, g):
         there = fulls[g].at[chips[k], core]
         return remote(there, there, fwd_sems, (k - 1, g), mate)
+
+    def attn_copy(k, g):
+        return remote(attn.at[others[k], span(g), :], attn_all.at[me, span(g), :], attn_sems, (k, g), others[k])
+
+    def project_out(g):
+        count = 8 * sizes[g]
+        mixed = attn_all.shape[2]
+        if g == 0:
+            attn_all[me] = attn[me]
+        for k in range(7):
+            attn_copy(k, g).wait_recv()
+
+        def tile(t, carry):
+            cols = pl.ds(pl.multiple_of(t * 512, 512), 512)
+            out = jnp.dot(act[:, span(g), :].reshape(count, act.shape[2]), w_buf[mixed:, cols], preferred_element_type=F32)
+            out = out + jnp.dot(attn_all[:, span(g), :].reshape(count, mixed), w_buf[:mixed, cols], preferred_element_type=F32)
+            part[:, :, span(g), cols] = out.astype(BF16).reshape(4, 2, sizes[g], 512)
+            return carry
+
+        lax.fori_loop(0, width // 512, tile, 0)
 
     def stat_copy(k):
         return remote(stat, stat_all.at[me], stat_sems, (k,), others[k])
@@ -386,7 +425,7 @@
         for k in (1, 2, 3):
             fwd_copy(k, g).wait_recv()
 
-    def logits(g, local_step, next_ref, tops):
+    def logits(g, local_step, tops):
         count = 8 * sizes[g]
         tile, sub = tiles[g], subs[g]
         z_rows = fulls[g][...].reshape(count, width)
@@ -398,7 +437,7 @@
             tops[2] = jnp.zeros_like(tops[2])
 
         top, acc, hit = tops[0], tops[1], tops[2]
-        wanted = next_ref[...] - local_step * tile - lax.broadcasted_iota(jnp.int32, (8, count), 0)
+        wanted = next_ref[:, 8 * offsets[g]:8 * offsets[g] + count] - local_step * tile - lax.broadcasted_iota(jnp.int32, (8, count), 0)
         for idx in range(tile // sub):
             dots = lax.dot_general(
                 e_ref[idx * sub:(idx + 1) * sub, :], z_rows, (((1,), (1,)), ((), ())), preferred_element_type=F32)
@@ -418,13 +457,21 @@
 
     @pl.when(step == 0)
     def _():
+        w_copy = pltpu.make_async_copy(w_ref, w_buf, w_sem)
+        w_copy.start()
         barrier = pltpu.get_barrier_semaphore()
         for target in others:
             pl.semaphore_signal(barrier, inc=1, device_id=(target,), device_id_type=MESH_ID)
         pl.semaphore_wait(barrier, 7)
+        for g in (0, 1):
+            for k in range(7):
+                attn_copy(k, g).start()
+        w_copy.wait()
+        project_out(0)
         pair_copy(0).start()
+        send_sums(0)
+        project_out(1)
         pair_copy(1).start()
-        send_sums(0)
         send_rows(0)
         send_sums(1)
         forward_rows(0)
@@ -440,7 +487,7 @@
 
     @pl.when(step < steps_a)
     def _():
-        logits(0, step, next_a, tops_a)
+        logits(0, step, tops_a)
 
     @pl.when(step == steps_a)
     def _():
@@ -448,7 +495,7 @@
 
     @pl.when(step >= steps_a)
     def _():
-        logits(1, step - steps_a, next_b, tops_b)
+        logits(1, step - steps_a, tops_b)
 
     @pl.when(step == last)
     def _():
@@ -475,6 +522,8 @@
         for k in range(7):
             stat_copy(k).wait_send()
         for g in (0, 1):
+            for k in range(7):
+                attn_copy(k, g).wait_send()
             pair_copy(g).wait_send()
             all_copy(0, g).wait_send()
             for k in (1, 2, 3):
@@ -483,22 +532,26 @@
                 fwd_copy(k, g).wait_send()
 
 
-def head(part, base, gain, local_next, embed_loc, cid, sizes=(32, 96), tiles=(3200, 3200), subs=(640, 640), when=(10, 4, 8)):
-    rows, width = part.shape
-    own_rows = rows // 8
+def head(attn, act, base, gain, local_next, w_out_loc, embed_loc, cid, sizes=(32, 96), tiles=(3200, 3200), subs=(640, 640), when=(10, 4, 8)):
+    own_rows, width = base.shape
+    rows = own_rows * 8
     vocab_dev = embed_loc.shape[0]
     steps_a, steps_b = vocab_dev // tiles[0], vocab_dev // tiles[1]
     vmem = pl.BlockSpec(memory_space=pltpu.VMEM)
     per_dev = local_next.reshape(8, own_rows)
-    wanted = [jnp.broadcast_to(ids.reshape(1, -1), (8, ids.size)) for ids in (per_dev[:, :sizes[0]], per_dev[:, sizes[0]:])]
+    wanted = jnp.concatenate([per_dev[:, :sizes[0]].reshape(-1), per_dev[:, sizes[0]:].reshape(-1)])
+    wanted = jnp.broadcast_to(wanted, (8, rows))
     dma = pltpu.SemaphoreType.DMA
     out = pl.pallas_call(
         functools.partial(head_kernel, sizes, tiles, subs, (steps_a,) + when[1:], width ** -0.5),
         grid=(steps_a + steps_b,),
-        in_specs=[vmem] * 5 + [pl.BlockSpec((tiles[0], width), lambda i: (lax.rem(i, steps_a), 0))],
+        in_specs=[vmem] * 5 + [pl.BlockSpec(memory_space=pl.ANY), pl.BlockSpec((tiles[0], width), lambda i: (lax.rem(i, steps_a), 0))],
         out_specs=vmem,
         out_shape=jax.ShapeDtypeStruct((1, rows), F32),
         scratch_shapes=[
+            pltpu.VMEM(w_out_loc.shape, BF16),
+            pltpu.VMEM(attn.shape, BF16),
+            pltpu.VMEM((4, 2, own_rows, width), BF16),
             pltpu.VMEM((4, 2, sizes[0], width), BF16),
             pltpu.VMEM((4, 2, sizes[1], width), BF16),
             pltpu.VMEM((4, own_rows, width), BF16),
@@ -508,11 +561,11 @@
             pltpu.VMEM((3, 8, 8 * sizes[1]), F32),
             pltpu.VMEM((8, rows), F32),
             pltpu.VMEM((8, 8, rows), F32),
-            dma((2, 2)), dma((2, 3, 2)), dma((2, 2)), dma((2, 3, 2)), dma((2, 3, 2)), dma((2, 7)),
+            dma, dma((2, 7, 2)), dma((2, 2)), dma((2, 3, 2)), dma((2, 2)), dma((2, 3, 2)), dma((2, 3, 2)), dma((2, 7)),
         ],
         compiler_params=pltpu.CompilerParams(collective_id=cid, has_side_effects=True, vmem_limit_bytes=63 * MIB),
         name="head_rows",
-    )(part.reshape(4, 2, own_rows, width), base, gain.reshape(1, width), *wanted, embed_loc)
+    )(attn, act, base, gain.reshape(1, width), wanted, w_out_loc, embed_loc)
     by_a = out[0, :8 * sizes[0]].reshape(8, sizes[0])
     by_b = out[0, 8 * sizes[0]:].reshape(8, sizes[1])
     return jnp.concatenate([by_a, by_b], axis=1)
@@ -562,12 +615,10 @@
         k_new = by_seq(rot[:, num_heads:].astype(BF16))
         v_new = by_seq(qkv_own[:, attn_width + head_dim:])
         attn_out, k_out, v_out = attention(own_lens, q_rot, k_new, v_new, k_loc, v_loc)
-        attn_out = attn_out.reshape(batch_dev, num_steps, attn_width).transpose(1, 0, 2).reshape(own_rows, attn_width)
-        attn_cols = lax.all_to_all(attn_out, 'tp', 1, 0, tiled=True)
-        mlp_act = mlp_act.reshape(group_size * own_rows, ff_dev)
-        combined = jnp.concatenate([attn_cols, mlp_act], axis=1)
-        part_out = jnp.dot(combined, w_out_loc, preferred_element_type=F32).astype(BF16)
-        logp = head(part_out, x_own, final_gain, to_rows(next_ids) - vocab_start, embed_loc, 1)
+        attn_parts = attn_out.reshape(batch_dev, num_steps, group_size, attn_dev).transpose(2, 1, 0, 3)
+        attn_parts = attn_parts.reshape(group_size, own_rows, attn_dev)
+        local_next = to_rows(next_ids) - vocab_start
+        logp = head(attn_parts, mlp_act, x_own, final_gain, local_next, w_out_loc, embed_loc, 1)
         logp = logp.reshape(group_size, num_steps, batch_dev).transpose(1, 0, 2).reshape(num_steps, batch_size)
         return logp, k_out, v_out
 

time: 330 us -> 301 us (0.912)
  matrix products: 15.1 us -> 0 us
  waiting for transfers between devices: 8.39 us -> 0 us
    dot_general x1 -> x0, matrix products: 15.1 us -> none  [device_fn(): jnp.dot(combined, w_out_loc, preferred_element_type=F32).astype(BF16)]
    all_to_all x1 -> x0, waiting for transfers between devices: 8.39 us -> none  [device_fn(): attn_cols = lax.all_to_all(attn_out, 'tp', 1, 0, tiled=True)]
    unnamed x7 -> x6, local copies, waits for them, and re-layouts: 4.48 us -> 0.01 us
    pallas_call x1, Pallas kernels: 13.4 us -> 9.78 us  [gather_rows(): pl.pallas_call(functools.partial(gather_kernel, count, vocab_dev), grid_s...]
  transfers between devices with their start and end apart: 1 -> 0, of which waited for: 1 -> 0; matrix products, arithmetic and copies ran while one was open for 0% -> 0% of each run, Pallas kernels for 0% -> 0%
where the time goes in v2:
time: 301 us
  Pallas kernels  286 us (95%)
  local copies, waits for them, and re-layouts  12.4 us (4%)
    pallas_call x1, Pallas kernels, head(): pl.pallas_call(functools.partial(head_kernel, sizes, tiles, subs, (steps_...  195 us
    pallas_call x1, Pallas kernels, project(): pl.pallas_call(functools.partial(project_kernel, chunks, qkv_dev, ff_dev)...  71 us
    pallas_call x1, Pallas kernels, attention(): pl.pallas_call(functools.partial(attention_kernel, seqs, steps, queries /...  9.91 us
    pallas_call x1, Pallas kernels, gather_rows(): pl.pallas_call(functools.partial(gather_kernel, count, vocab_dev), grid_s...  9.78 us

profile of v2, /device:TPU:0, one launch (start us, length us, event | category | flops | bytes accessed | tf_op | source)
XLA Modules:
  0.0 300.6 jit_solution(14703801527832806289)
XLA Ops:
  0.6 0.8 dynamic_slice.3.lens_ref
  1.4 0.0 copy-start.2
  1.4 0.1 convert_element_type.23
  1.5 0.3 multiply_cosine_fusion
  1.8 0.7 broadcast_subtract_fusion
  2.5 0.1 sub.31
  2.6 0.7 sub.33.ids_ref
  3.3 0.0 copy-start
  3.3 9.8 %gather_rows.1 = bf16[1024,2048]{1,0:T(8,128)(2,1)} custom-call(s32[1024]{0:T(1024)} %sub.33.ids_ref, bf16[32000,2048]{1,0:T(8,128)(2,1)} %refs_6_.1), custom_call_target="tpu_custom_call" | custom-call | tf_op jit(solution)/shard_map/gather_rows/pallas_call | solution.py:74
  13.1 0.0 copy-done.2
  13.1 0.0 copy-done
  13.1 0.6 reshape.141.refs_1_
  13.7 71.0 %project_rows.1 = (bf16[128,2048]{1,0:T(8,128)(2,1)}, bf16[8,128,2048]{2,1,0:T(8,128)(2,1)}, bf16[8,128,320]{2,1,0:T(8,128)(2,1)}) custom-call(bf16[4,2,128,2048]{3,2,1,0:T(8,128)(2,1)} %bitcast.39, bf16[1,2048]{1,0:T(2,128)(2,1)} %reshape.141.refs_1_, bf16[4416,2048]{1,0:T(8,128)(2,1)} %bitcast.38), custom_call_target="tpu_custom_call" | custom-call | tf_op jit(solution)/shard_map/project_rows/pallas_call | solution.py:255
  84.7 1.5 copy.16
  86.2 0.1 convert.5
  86.3 0.2 multiply_add_fusion
  86.5 0.1 copy.19
  86.6 0.7 copy.34
  87.3 0.1 fusion.2
  87.4 0.4 copy.17
  87.8 0.8 copy.32
  88.7 0.1 copy.21
  88.8 0.7 copy.33
  89.5 0.0 copy-start.1
  89.5 9.9 %attention_rows.1 = (bf16[64,16,256]{2,1,0:T(8,128)(2,1)}, bf16[64,128,256]{2,1,0:T(8,128)(2,1)}, bf16[64,128,256]{2,1,0:T(8,128)(2,1)}) custom-call(s32[64]{0:T(128)} %copy-done.2, bf16[64,16,256]{2,1,0:T(8,128)(2,1)} %bitcast.44, bf16[64,2,256]{2,1,0:T(2,128)(2,1)} %bitcast.48, bf16[64,2,256]{2,1,0:T(2,128)(2,1)} %bitcast.49, bf16[64,128,256]{2,1,0:T(8,128)(2,1)} %k_ref.1, ...), custom_call_target="tpu_custom_call" | custom-call | tf_op jit(solution)/shard_map/attention_rows/pallas_call | solution.py:321
  99.4 2.0 copy.23
  101.4 0.1 sub.36
  101.5 0.1 sub.38
  101.5 0.1 slice.38
  101.6 0.1 reshape.153
  101.7 0.1 reshape.152
  101.8 0.6 broadcast_in_dim.2.refs_4_
  102.4 0.0 copy-done.1
  102.4 0.6 reshape.151.refs_3_
  103.0 195.3 %head_rows.1 = f32[1,1024]{1,0:T(1,128)} custom-call(bf16[8,128,256]{2,1,0:T(8,128)(2,1)} %bitcast.43, bf16[8,128,2048]{2,1,0:T(8,128)(2,1)} %get-tuple-element.11.refs_1_, bf16[128,2048]{1,0:T(8,128)(2,1)} %get-tuple-element.12.refs_2_, bf16[1,2048]{1,0:T(2,128)(2,1)} %reshape.151.refs_3_, s32[8,1024]{1,0:T(8,128)} %broadcast_in_dim.2.refs_4_, ...), custom_call_target="tpu_custom_call" | custom-call | tf_op jit(solution)/shard_map/head_rows/pallas_call | solution.py:545
  298.3 0.7 slice_reduce_fusion
  299.0 0.1 reshape_squeeze.7
  299.0 0.7 slice_reduce_fusion.1
  299.7 0.1 reshape_squeeze.6
  299.8 0.1 pad_maximum_fusion.1
  299.9 0.1 reshape.154
  300.0 0.7 reshape.155
  (9 shorter events, 0.1 us)
Async XLA Ops:
  1.4 11.7 %copy-start.2 = (s32[64]{0:T(128)}, s32[64]{0:T(128)S(1)}, u32[]{:S(2)}) copy-start(s32[64]{0:T(128)S(1)} %dynamic_slice.3.lens_ref) | copy-start | bytes 772
  3.3 9.8 %copy-start = (bf16[2048]{0:T(1024)(128)(2,1)S(1)}, bf16[2048]{0:T(1024)(128)(2,1)}, u32[]{:S(2)}) copy-start(bf16[2048]{0:T(1024)(128)(2,1)} %param.14) | copy-start | bytes 12292
  89.5 12.9 %copy-start.1 = (bf16[2048]{0:T(1024)(128)(2,1)S(1)}, bf16[2048]{0:T(1024)(128)(2,1)}, u32[]{:S(2)}) copy-start(bf16[2048]{0:T(1024)(128)(2,1)} %param.17) | copy-start | bytes 12292

commit v3 on v2

--- a/solution.py
+++ b/solution.py
@@ -336,9 +336,9 @@
     )(own_lens, q_rot, k_new, v_new, k_loc, v_loc)
 
 
-def head_kernel(sizes, tiles, subs, when, scale, *refs):
-    (attn, act, base, gain, next_ref, w_ref, e_ref, out_ref, w_buf, attn_all, part, full_a, full_b, pair_buf, send_buf, recv_buf, tops_a, tops_b,
-     stat, stat_all, w_sem, attn_sems, pair_sems, sum_sems, own_sems, all_sems, fwd_sems, stat_sems) = refs
+def head_kernel(sizes, tile, subs, tile_count, when, scale, *refs):
+    (attn, base, gain, next_ref, act_ref, w_ref, e_ref, out_ref, e_buf, act, w_buf, attn_all, part, full_a, full_b, pair_buf, send_buf, recv_buf, tops_a, tops_b,
+     stat, stat_all, e_sems, act_sem, w_sem, attn_sems, pair_sems, sum_sems, own_sems, all_sems, fwd_sems, stat_sems) = refs
     step = pl.program_id(0)
     me = lax.axis_index("tp")
     chip, core = me // 2, lax.rem(me, 2)
@@ -425,40 +425,48 @@
         for k in (1, 2, 3):
             fwd_copy(k, g).wait_recv()
 
-    def logits(g, local_step, tops):
+    def tile_copy(at):
+        start = pl.multiple_of(lax.rem(at, tile_count) * tile, tile)
+        return pltpu.make_async_copy(e_ref.at[pl.ds(start, tile), :], e_buf.at[lax.rem(at, 2)], e_sems.at[lax.rem(at, 2)])
+
+    def logits(g, first, tops):
         count = 8 * sizes[g]
-        tile, sub = tiles[g], subs[g]
+        sub = subs[g]
+        slot = lax.rem(step, 2)
         z_rows = fulls[g][...].reshape(count, width)
 
-        @pl.when(local_step == 0)
+        @pl.when(step == first)
         def _():
             tops[0] = jnp.full_like(tops[0], -jnp.inf)
             tops[1] = jnp.zeros_like(tops[1])
             tops[2] = jnp.zeros_like(tops[2])
 
         top, acc, hit = tops[0], tops[1], tops[2]
-        wanted = next_ref[:, 8 * offsets[g]:8 * offsets[g] + count] - local_step * tile - lax.broadcasted_iota(jnp.int32, (8, count), 0)
+        wanted = next_ref[:, 8 * offsets[g]:8 * offsets[g] + count] - lax.rem(step, tile_count) * tile - lax.broadcasted_iota(jnp.int32, (8, count), 0)
         for idx in range(tile // sub):
             dots = lax.dot_general(
-                e_ref[idx * sub:(idx + 1) * sub, :], z_rows, (((1,), (1,)), ((), ())), preferred_element_type=F32)
+                e_buf[slot, idx * sub:(idx + 1) * sub, :], z_rows, (((1,), (1,)), ((), ())), preferred_element_type=F32)
             dots = dots.reshape(sub // 8, 8, count)
             new_top = jnp.maximum(top, jnp.max(dots, axis=0))
             acc = acc * jnp.exp2((top - new_top) * (scale * LOG2E)) + jnp.sum(
                 jnp.exp2((dots - new_top[None]) * (scale * LOG2E)), axis=0)
             top = new_top
             for row in range(sub // 8):
-                hit = hit + jnp.where(wanted == idx * sub + row * 8, dots[row], 0.0)
+                hit = jnp.where(wanted == idx * sub + row * 8, dots[row], hit)
         tops[0] = top
         tops[1] = acc
         tops[2] = hit
 
-    steps_a = when[0]
     last = pl.num_programs(0) - 1
 
     @pl.when(step == 0)
     def _():
         w_copy = pltpu.make_async_copy(w_ref, w_buf, w_sem)
         w_copy.start()
+        act_copy = pltpu.make_async_copy(act_ref, act, act_sem)
+        act_copy.start()
+        tile_copy(0).start()
+        tile_copy(1).start()
         barrier = pltpu.get_barrier_semaphore()
         for target in others:
             pl.semaphore_signal(barrier, inc=1, device_id=(target,), device_id_type=MESH_ID)
@@ -467,6 +475,7 @@
             for k in range(7):
                 attn_copy(k, g).start()
         w_copy.wait()
+        act_copy.wait()
         project_out(0)
         pair_copy(0).start()
         send_sums(0)
@@ -477,25 +486,31 @@
         forward_rows(0)
         rows_here(0)
 
+    @pl.when(step == when[0])
+    def _():
+        send_rows(1)
+
     @pl.when(step == when[1])
     def _():
-        send_rows(1)
+        forward_rows(1)
 
     @pl.when(step == when[2])
     def _():
-        forward_rows(1)
-
-    @pl.when(step < steps_a)
-    def _():
-        logits(0, step, tops_a)
-
-    @pl.when(step == steps_a)
-    def _():
         rows_here(1)
 
-    @pl.when(step >= steps_a)
-    def _():
-        logits(1, step - steps_a, tops_b)
+    tile_copy(step).wait()
+
+    @pl.when(step < tile_count)
+    def _():
+        logits(0, 0, tops_a)
+
+    @pl.when(step >= when[2])
+    def _():
+        logits(1, when[2], tops_b)
+
+    @pl.when(step + 2 <= last)
+    def _():
+        tile_copy(step + 2).start()
 
     @pl.when(step == last)
     def _():
@@ -532,23 +547,25 @@
                 fwd_copy(k, g).wait_send()
 
 
-def head(attn, act, base, gain, local_next, w_out_loc, embed_loc, cid, sizes=(32, 96), tiles=(3200, 3200), subs=(640, 640), when=(10, 4, 8)):
+def head(attn, act, base, gain, local_next, w_out_loc, embed_loc, cid, sizes=(32, 96), tile=3200, subs=(640, 640), when=(4, 7, 8)):
     own_rows, width = base.shape
     rows = own_rows * 8
     vocab_dev = embed_loc.shape[0]
-    steps_a, steps_b = vocab_dev // tiles[0], vocab_dev // tiles[1]
+    tile_count = vocab_dev // tile
     vmem = pl.BlockSpec(memory_space=pltpu.VMEM)
     per_dev = local_next.reshape(8, own_rows)
     wanted = jnp.concatenate([per_dev[:, :sizes[0]].reshape(-1), per_dev[:, sizes[0]:].reshape(-1)])
     wanted = jnp.broadcast_to(wanted, (8, rows))
     dma = pltpu.SemaphoreType.DMA
     out = pl.pallas_call(
-        functools.partial(head_kernel, sizes, tiles, subs, (steps_a,) + when[1:], width ** -0.5),
-        grid=(steps_a + steps_b,),
-        in_specs=[vmem] * 5 + [pl.BlockSpec(memory_space=pl.ANY), pl.BlockSpec((tiles[0], width), lambda i: (lax.rem(i, steps_a), 0))],
+        functools.partial(head_kernel, sizes, tile, subs, tile_count, when, width ** -0.5),
+        grid=(tile_count + when[2],),
+        in_specs=[vmem] * 4 + [pl.BlockSpec(memory_space=pl.ANY)] * 3,
         out_specs=vmem,
         out_shape=jax.ShapeDtypeStruct((1, rows), F32),
         scratch_shapes=[
+            pltpu.VMEM((2, tile, width), BF16),
+            pltpu.VMEM(act.shape, BF16),
             pltpu.VMEM(w_out_loc.shape, BF16),
             pltpu.VMEM(attn.shape, BF16),
             pltpu.VMEM((4, 2, own_rows, width), BF16),
@@ -561,11 +578,11 @@
             pltpu.VMEM((3, 8, 8 * sizes[1]), F32),
             pltpu.VMEM((8, rows), F32),
             pltpu.VMEM((8, 8, rows), F32),
-            dma, dma((2, 7, 2)), dma((2, 2)), dma((2, 3, 2)), dma((2, 2)), dma((2, 3, 2)), dma((2, 3, 2)), dma((2, 7)),
+            dma((2,)), dma, dma, dma((2, 7, 2)), dma((2, 2)), dma((2, 3, 2)), dma((2, 2)), dma((2, 3, 2)), dma((2, 3, 2)), dma((2, 7)),
         ],
         compiler_params=pltpu.CompilerParams(collective_id=cid, has_side_effects=True, vmem_limit_bytes=63 * MIB),
         name="head_rows",
-    )(attn, act, base, gain.reshape(1, width), wanted, w_out_loc, embed_loc)
+    )(attn, base, gain.reshape(1, width), wanted, act, w_out_loc, embed_loc)
     by_a = out[0, :8 * sizes[0]].reshape(8, sizes[0])
     by_b = out[0, 8 * sizes[0]:].reshape(8, sizes[1])
     return jnp.concatenate([by_a, by_b], axis=1)

time: 301 us -> 300 us (level)
  no operation moved by 1% of the time
where the time goes in v3:
time: 300 us
  Pallas kernels  285 us (95%)
  local copies, waits for them, and re-layouts  12.4 us (4%)
    pallas_call x1, Pallas kernels, head(): pl.pallas_call(functools.partial(head_kernel, sizes, tile, subs, tile_cou...  195 us
    pallas_call x1, Pallas kernels, project(): pl.pallas_call(functools.partial(project_kernel, chunks, qkv_dev, ff_dev)...  69.8 us
    pallas_call x1, Pallas kernels, gather_rows(): pl.pallas_call(functools.partial(gather_kernel, count, vocab_dev), grid_s...  10.7 us
    pallas_call x1, Pallas kernels, attention(): pl.pallas_call(functools.partial(attention_kernel, seqs, steps, queries /...  9.91 us

profile of v3, /device:TPU:0, one launch (start us, length us, event | category | flops | bytes accessed | tf_op | source)
XLA Modules:
  0.0 299.8 jit_solution(13285907075887518239)
XLA Ops:
  0.6 0.8 dynamic_slice.3.lens_ref
  1.4 0.0 copy-start.2
  1.4 0.1 convert_element_type.23
  1.5 0.3 multiply_cosine_fusion
  1.8 0.7 broadcast_subtract_fusion
  2.5 0.1 sub.31
  2.6 0.7 sub.33.ids_ref
  3.3 0.0 copy-start
  3.3 10.7 %gather_rows.1 = bf16[1024,2048]{1,0:T(8,128)(2,1)} custom-call(s32[1024]{0:T(1024)} %sub.33.ids_ref, bf16[32000,2048]{1,0:T(8,128)(2,1)} %refs_6_.1), custom_call_target="tpu_custom_call" | custom-call | tf_op jit(solution)/shard_map/gather_rows/pallas_call | solution.py:74
  14.0 0.0 copy-done.2
  14.0 0.0 copy-done
  14.1 0.6 reshape.141.refs_1_
  14.7 69.8 %project_rows.1 = (bf16[128,2048]{1,0:T(8,128)(2,1)}, bf16[8,128,2048]{2,1,0:T(8,128)(2,1)}, bf16[8,128,320]{2,1,0:T(8,128)(2,1)}) custom-call(bf16[4,2,128,2048]{3,2,1,0:T(8,128)(2,1)} %bitcast.39, bf16[1,2048]{1,0:T(2,128)(2,1)} %reshape.141.refs_1_, bf16[4416,2048]{1,0:T(8,128)(2,1)} %bitcast.38), custom_call_target="tpu_custom_call" | custom-call | tf_op jit(solution)/shard_map/project_rows/pallas_call | solution.py:255
  84.4 1.5 copy.16
  86.0 0.1 convert.5
  86.1 0.2 multiply_add_fusion
  86.3 0.1 copy.19
  86.4 0.7 copy.34
  87.1 0.1 fusion.2
  87.2 0.4 copy.17
  87.6 0.8 copy.32
  88.4 0.1 copy.21
  88.5 0.7 copy.33
  89.2 0.0 copy-start.1
  89.2 9.9 %attention_rows.1 = (bf16[64,16,256]{2,1,0:T(8,128)(2,1)}, bf16[64,128,256]{2,1,0:T(8,128)(2,1)}, bf16[64,128,256]{2,1,0:T(8,128)(2,1)}) custom-call(s32[64]{0:T(128)} %copy-done.2, bf16[64,16,256]{2,1,0:T(8,128)(2,1)} %bitcast.44, bf16[64,2,256]{2,1,0:T(2,128)(2,1)} %bitcast.48, bf16[64,2,256]{2,1,0:T(2,128)(2,1)} %bitcast.49, bf16[64,128,256]{2,1,0:T(8,128)(2,1)} %k_ref.1, ...), custom_call_target="tpu_custom_call" | custom-call | tf_op jit(solution)/shard_map/attention_rows/pallas_call | solution.py:321
  99.1 2.0 copy.23
  101.1 0.1 sub.36
  101.2 0.1 sub.38
  101.3 0.1 slice.38
  101.4 0.1 reshape.153
  101.4 0.1 reshape.152
  101.5 0.6 broadcast_in_dim.2.refs_3_
  102.1 0.0 copy-done.1
  102.1 0.6 reshape.151.refs_2_
  102.7 194.7 %head_rows.1 = f32[1,1024]{1,0:T(1,128)} custom-call(bf16[8,128,256]{2,1,0:T(8,128)(2,1)} %bitcast.43, bf16[128,2048]{1,0:T(8,128)(2,1)} %get-tuple-element.11.refs_1_, bf16[1,2048]{1,0:T(2,128)(2,1)} %reshape.151.refs_2_, s32[8,1024]{1,0:T(8,128)} %broadcast_in_dim.2.refs_3_, bf16[8,128,2048]{2,1,0:T(8,128)(2,1)} %get-tuple-element.12.refs_4_, ...), custom_call_target="tpu_custom_call" | custom-call | tf_op jit(solution)/shard_map/head_rows/pallas_call | solution.py:560
  297.4 0.7 slice_reduce_fusion
  298.1 0.1 reshape_squeeze.7
  298.2 0.7 slice_reduce_fusion.1
  298.9 0.1 reshape_squeeze.6
  298.9 0.1 pad_maximum_fusion.1
  299.0 0.1 reshape.154
  299.1 0.7 reshape.155
  (9 shorter events, 0.1 us)
Async XLA Ops:
  1.4 12.6 %copy-start.2 = (s32[64]{0:T(128)}, s32[64]{0:T(128)S(1)}, u32[]{:S(2)}) copy-start(s32[64]{0:T(128)S(1)} %dynamic_slice.3.lens_ref) | copy-start | bytes 772
  3.3 10.8 %copy-start = (bf16[2048]{0:T(1024)(128)(2,1)S(1)}, bf16[2048]{0:T(1024)(128)(2,1)}, u32[]{:S(2)}) copy-start(bf16[2048]{0:T(1024)(128)(2,1)} %param.14) | copy-start | bytes 12292
  89.2 12.9 %copy-start.1 = (bf16[2048]{0:T(1024)(128)(2,1)S(1)}, bf16[2048]{0:T(1024)(128)(2,1)}, u32[]{:S(2)}) copy-start(bf16[2048]{0:T(1024)(128)(2,1)} %param.17) | copy-start | bytes 12292
